TPU v7x, 256 devices: a 4x2x16 block of a 4x16x16 slice. The times are simulated.
256 devices in a mesh: group: 2 (over y), temp: 4 (over x), gz: 32 (over z, core).
Axes of the slice: x: 4, y: 2, z: 16, core: 2. Of those that a mesh axis runs over, the one named last changes fastest.
The devices are a block of a 4x16x16 slice.
Arguments:
- spin_state: float32 [16, 3, 128, 128, 128], P(('group', 'temp'), None, 'gz'), parts along dimension 0, may hold values from -1 to 1, as said below
- couplings: float32 [3, 256, 128, 128], P(None, ('group', 'gz')), parts along dimension 1, may hold values from -12 to 12
- inverse_temps: float32 [16], P(('group', 'temp')), parts along dimension 0, may hold values from 0.3 to 3
- colour_order: int32 [16], P(('group', 'temp')), parts along dimension 0, may hold values 0 or 1
- heat_level: float32 [16, 128, 128, 128], P(('group', 'temp'), 'gz'), parts along dimension 0, may hold values from 0.001 to 0.999
- heat_height: float32 [16, 128, 128, 128], P(('group', 'temp'), 'gz'), parts along dimension 0, may hold values from -1 to 1
- heat_angle: float32 [16, 128, 128, 128], P(('group', 'temp'), 'gz'), parts along dimension 0, may hold values from -3.140625 to 3.140625
- swap_bits: int32 [16], P(('group', 'temp')), parts along dimension 0, may hold values 0 or 1
Outputs:
- spin_final: float32 [16, 3, 128, 128, 128], P(('group', 'temp'), None, 'gz'), parts along dimension 0
- energies: float32 [16], P(('group', 'temp')), parts along dimension 0
There are 2 independent parts, one for each index of `group`. A program takes and returns all parts, laid end to end along the dimension named above; each array names one. Nothing has to cross between parts.
Inputs may be any that keep to these rules, and one draw needn't show every extreme that they name: `spin_state`: every site's three components form a vector of unit length.
All inputs are finite; a program needn't handle non-finite values. No bound on the sum of `colour_order` or of `swap_bits` on one device may be relied on, other than what follows from the above.
Results may differ from a plain program's by a relative error of at most 0.0003.
Values sent between devices are 32-bit elements; how exact they have to be, the bound alone decides.
No kernel may reach another device: no remote copies, remote signals or barrier semaphores. Data moves between devices by JAX's collectives and lax.ppermute only.
A program may use at most 64 MiB of HBM per device.

v0:
```python
import functools

import jax
import jax.numpy as jnp
from jax import lax
from jax.experimental import pallas as pl
from jax.experimental.pallas import tpu as pltpu
from jax.sharding import PartitionSpec as P


F32 = jnp.float32
OR_SWEEPS = 2


VM = pl.BlockSpec(memory_space=pltpu.VMEM)
SM = pl.BlockSpec(memory_space=pltpu.SMEM)
ANY = pl.BlockSpec(memory_space=pl.ANY)
HBM = pl.BlockSpec(memory_space=pltpu.HBM)
PIECES = 9


def vm(*shape, dtype=F32):
    return pltpu.VMEM(shape, dtype)


def kernel_call(body, outs, in_specs, out_specs=None, scratch=(), mib=24):
    return pl.pallas_call(
        body,
        out_shape=outs,
        in_specs=in_specs,
        out_specs=out_specs if out_specs is not None else [VM] * len(outs),
        scratch_shapes=list(scratch),
        compiler_params=pltpu.CompilerParams(vmem_limit_bytes=mib * 1024 * 1024),
    )


def in_hbm(value):
    return pltpu.with_memory_space_constraint(value, pltpu.HBM)


def core_index():
    return lax.rem(lax.axis_index("gz"), 2)


def slot_replica(swap, slot):
    bit = (swap[0] != 0).astype(jnp.int32)
    return bit if slot == 0 else 1 - bit


def lane_even(rows, columns, offset):
    lane = lax.broadcasted_iota(jnp.int32, (rows, columns), 1)
    return ((lane + offset) & 1) == 0


def tile(ref, i, half):
    return ref[pl.ds(i * half, half), :]


def put(ref, i, value):
    half = value.shape[0]
    ref[pl.ds(i * half, half), :] = value


def folded(ref, index, half):
    return tuple(ref[(*index, pl.ds(s, half, stride=2), slice(None))] for s in (0, 1))


def folded_rows(ref, base, half):
    return tuple(ref[pl.ds(base + s, half, stride=2), :] for s in (0, 1))


def parity(info, half):
    columns = info.shape[-1]
    lane = lax.broadcasted_iota(jnp.int32, (half, columns), 1)
    return (lane & 1) == jnp.broadcast_to(info[0:1, :], (half, columns))


def at_plane(even, w):
    return even if w % 2 == 0 else jnp.logical_not(even)


def load_kernel(planes, half, *refs):
    (swap_h, colour_h, beta_h, spin_h, coup_h) = refs[:5]
    (p1x, p1i, p0x, p0i, am0, am1, info0, info1, beta0, beta1) = refs[5:15]
    swap, colour, betas, spin, sems = refs[15:]
    core = core_index()
    columns = spin.shape[-1]
    rows = 2 * half
    top = planes - 1
    copies = [
        pltpu.make_async_copy(swap_h, swap, sems.at[0]),
        pltpu.make_async_copy(colour_h, colour, sems.at[1]),
        pltpu.make_async_copy(beta_h, betas, sems.at[2]),
        pltpu.make_async_copy(spin_h, spin, sems.at[3]),
    ]
    zx = core * top
    zi = top - zx
    for ref, z, near, outer, sem in (
        (p1x, zx, core * (top - 1), zx, 4),
        (p1i, zi, (1 - core) * (top - 1), zi, 8),
    ):
        for i, (d, p) in enumerate(((0, z), (1, z), (2, near), (2, outer))):
            target = ref.at[pl.ds(PIECES * half + i * rows, rows), :]
            copies.append(pltpu.make_async_copy(coup_h.at[d, p], target, sems.at[sem + i]))
    for copy in copies:
        copy.start()
    for copy in copies[:4]:
        copy.wait()
    for slot, sx, si, am, info, beta in (
        (1, p1x, p1i, am1, info1, beta1),
        (0, p0x, p0i, am0, info0, beta0),
    ):
        rep = slot_replica(swap, slot)
        c = colour[rep]
        info[0:1, :] = jnp.full((1, columns), c ^ core, jnp.int32)
        info[1:2, :] = jnp.full((1, columns), (swap[1] != 0).astype(jnp.int32), jnp.int32)
        beta[...] = jnp.full(beta.shape, betas[rep], F32)
        for w in range(planes):
            z = w + core * (top - 2 * w)
            m = lane_even(half, columns, z + c)
            for k in range(3):
                even, odd = folded(spin, (rep, k, z), half)
                a = jnp.where(m, even, odd)
                b = jnp.where(m, odd, even)
                if w == 0:
                    put(sx, k, b)
                    put(sx, 6 + k, a)
                elif w == 1:
                    put(sx, 3 + k, b)
                    put(am, k, a)
                elif w == planes - 2:
                    put(si, 3 + k, b)
                    put(am, 3 + k, a)
                else:
                    put(si, k, b)
                    put(si, 6 + k, a)
    for copy in copies[4:]:
        copy.wait()


def weight_kernel(planes, half, coup, rcx, rci, info0, info1, weights0, weights1):
    core = core_index()
    top = planes - 1
    rows = 2 * half
    first = core == 0

    def sent(ref, i):
        return folded_rows(ref, PIECES * half + i * rows, half)

    def zbond(m):
        if m == -1:
            return sent(rcx, 2)
        if m == planes + 1:
            return sent(rci, 2)
        if m == 0:
            ours, theirs = folded(coup, (2, top), half), sent(rcx, 3)
            return tuple(jnp.where(first, t, o) for o, t in zip(ours, theirs))
        if m == planes:
            ours, theirs = folded(coup, (2, top), half), sent(rci, 3)
            return tuple(jnp.where(first, o, t) for o, t in zip(ours, theirs))
        return folded(coup, (2, (m - 1) + core * (top - 2 * m + 1)), half)

    below = zbond(-1)
    for w in range(-1, planes + 1):
        above = zbond(w + 1)
        if w == -1:
            jx, jy = sent(rcx, 0), sent(rcx, 1)
        elif w == planes:
            jx, jy = sent(rci, 0), sent(rci, 1)
        else:
            z = w + core * (top - 2 * w)
            jx, jy = folded(coup, (0, z), half), folded(coup, (1, z), half)
        up_odd = pltpu.roll(jy[1], 1, 0)
        for info, weights in ((info0, weights0), (info1, weights1)):
            even = parity(info, half)
            for a in (0, 1):
                if a == 1 and (w == -1 or w == planes):
                    continue
                m = at_plane(even, w + a)
                weights[a, w + 1, 0] = jnp.where(m, jx[0], jx[1])
                weights[a, w + 1, 1] = pltpu.roll(jnp.where(m, jx[1], jx[0]), 1, 1)
                weights[a, w + 1, 2] = jy[0]
                weights[a, w + 1, 3] = jnp.where(m, up_odd, jy[1])
                weights[a, w + 1, 4] = jnp.where(m, above[0], above[1])
                weights[a, w + 1, 5] = jnp.where(m, below[0], below[1])
        below = above


def field(get, weights, a, even, w):
    total = []
    m = at_plane(even, w + a)
    for k in range(3):
        o = get(w, k)
        half, columns = o.shape
        side = jnp.where(m, pltpu.roll(o, 1, 0), pltpu.roll(o, half - 1, 0))
        h = weights[a, w + 1, 0] * pltpu.roll(o, columns - 1, 1)
        h = h + weights[a, w + 1, 1] * pltpu.roll(o, 1, 1)
        h = h + weights[a, w + 1, 2] * o
        h = h + weights[a, w + 1, 3] * side
        h = h + weights[a, w + 1, 4] * get(w + 1, k)
        h = h + weights[a, w + 1, 5] * get(w - 1, k)
        total.append(h)
    return total


def dot3(a, b):
    return a[0] * b[0] + a[1] * b[1] + a[2] * b[2]


def reflect(s, h):
    f = 2.0 * dot3(s, h) / jnp.maximum(dot3(h, h), 0.01)
    return [f * h[k] - s[k] for k in range(3)]


def second_planes(planes, half, sx, si, rx, ri):
    def get(w, k):
        if w < 0:
            return tile(rx, 3 * (-1 - w) + k, half)
        if w < 2:
            return tile(sx, 3 * w + k, half)
        if w < planes:
            return tile(si, 3 * (planes - 1 - w) + k, half)
        return tile(ri, 3 * (w - planes) + k, half)

    return get


def relax_kernel(planes, half, first, *refs):
    info, weights, sx, si, rx, ri, a_old = refs[:7]
    a_new, bx, bi = refs[7:] if first else (refs[9], refs[7], refs[8])
    even = parity(info, half)
    get_b = second_planes(planes, half, sx, si, rx, ri)

    def get_a(w, k):
        if not first:
            return a_old[w + 1, k]
        if w == -1:
            return tile(rx, 6 + k, half)
        if w == 0:
            return tile(sx, 6 + k, half)
        if w == planes - 1:
            return tile(si, 6 + k, half)
        if w == planes:
            return tile(ri, 6 + k, half)
        return tile(a_old, 3 * (w - 1) + k, half)

    for w in range(-1, planes + 1):
        h = field(get_b, weights, 0, even, w)
        new = reflect([get_a(w, k) for k in range(3)], h)
        for k in range(3):
            a_new[w + 1, k] = new[k]
    for w in range(planes):
        h = field(lambda v, k: a_new[v + 1, k], weights, 1, even, w)
        new = reflect([get_b(w, k) for k in range(3)], h)
        for k in range(3):
            if w < 2:
                put(bx, 3 * w + k, new[k])
            else:
                put(bi, 3 * (planes - 1 - w) + k, new[k])


SIN = (1.0, -1 / 6, 1 / 120, -1 / 5040, 1 / 362880, -1 / 39916800, 1 / 6227020800)
COS = (1.0, -1 / 2, 1 / 24, -1 / 720, 1 / 40320, -1 / 3628800, 1 / 479001600, -1 / 87178291200)


def series(coefficients, y):
    total = coefficients[-1]
    for value in coefficients[-2::-1]:
        total = total * y + value
    return total


def trial(height, angle):
    t = 0.5 * angle
    y = t * t
    s = t * series(SIN, y)
    c = series(COS, y)
    q = jnp.sqrt(jnp.maximum(1.0 - height * height, 0.0))
    return q * (1.0 - 2.0 * (s * s)), q * (2.0 * (s * c))


def trial_kernel(planes, half, swap, colour, level, height, angle, ta0, tb0, ta1, tb1, dx, di):
    core = core_index()
    columns = level.shape[-1]
    for slot, ta, tb in ((0, ta0, tb0), (1, ta1, tb1)):
        rep = slot_replica(swap, slot)
        c = colour[rep]
        for w in range(planes):
            z = w + core * (planes - 1 - 2 * w)
            m = lane_even(half, columns, z + c)
            a, b = [], []
            for ref in (level, height, angle):
                even, odd = folded(ref, (rep, z), half)
                a.append(jnp.where(m, even, odd))
                b.append(jnp.where(m, odd, even))
            if w == 0 or w == planes - 1:
                for i in range(3):
                    put(dx if w == 0 else di, 3 * slot + i, a[i])
            for t, (lev, hei, ang) in ((ta, a), (tb, b)):
                ux, uy = trial(hei, ang)
                t[w, 0], t[w, 1], t[w, 2], t[w, 3] = ux, uy, hei, lev


def heated(h, u, level, beta):
    m = jnp.maximum(dot3(h, h), 0.01)
    inverse = lax.rsqrt(m)
    e = [h[k] * inverse for k in range(3)]
    reach = beta * (m * inverse)
    c = 1.0 + jnp.log(1.0 + level * (jnp.exp(-2.0 * reach) - 1.0)) / reach
    along = dot3(u, e)
    t = [u[k] - along * e[k] for k in range(3)]
    f = jnp.sqrt(jnp.maximum(1.0 - c * c, 0.0)) * lax.rsqrt(jnp.maximum(dot3(t, t), 0.0001))
    return [c * e[k] + f * t[k] for k in range(3)]


def inner_kernel(planes, half, info, betas, weights, sx, si, ta, out):
    even = parity(info, half)
    columns = info.shape[-1]
    beta = jnp.broadcast_to(betas[0:1, :], (half, columns))
    get_b = second_planes(planes, half, sx, si, None, None)
    for w in range(1, planes - 1):
        h = field(get_b, weights, 0, even, w)
        new = heated(h, [ta[w, k] for k in range(3)], ta[w, 3], beta)
        for k in range(3):
            put(out, 3 * (w - 1) + k, new[k])
    out[pl.ds(3 * (planes - 2) * half, 8), :] = info[...].astype(F32)


def heat_kernel(planes, half, slot, *refs):
    info, betas, weights, sx, si, rx, ri, ta, tb, rdx, rdi, inner, out, e_out, ah = refs
    even = parity(info, half)
    columns = info.shape[-1]
    beta = jnp.broadcast_to(betas[0:1, :], (half, columns))
    get_b = second_planes(planes, half, sx, si, rx, ri)

    def get_a(w, k):
        if w < 0:
            return ah[0, k]
        if w == planes:
            return ah[1, k]
        if w == 0:
            return tile(out, k, half)
        if w == planes - 1:
            return tile(out, 3 + k, half)
        return tile(inner, 3 * (w - 1) + k, half)

    for w in (-1, 0, planes - 1, planes):
        h = field(get_b, weights, 0, even, w)
        if 0 <= w < planes:
            u, level = [ta[w, k] for k in range(3)], ta[w, 3]
        else:
            d = rdx if w < 0 else rdi
            height = tile(d, 3 * slot + 1, half)
            ux, uy = trial(height, tile(d, 3 * slot + 2, half))
            u, level = [ux, uy, height], tile(d, 3 * slot, half)
        new = heated(h, u, level, beta)
        for k in range(3):
            if w < 0:
                ah[0, k] = new[k]
            elif w == planes:
                ah[1, k] = new[k]
            else:
                put(out, (0 if w == 0 else 3) + k, new[k])
    energy = None
    for w in range(planes):
        h = field(get_a, weights, 1, even, w)
        new = heated(h, [tb[w, k] for k in range(3)], tb[w, 3], beta)
        for k in range(3):
            put(out, 6 + 3 * w + k, new[k])
        term = dot3(new, h)
        energy = term if energy is None else energy + term
    e_out[...] = jnp.full(e_out.shape, -jnp.sum(energy), F32)


def decide_kernel(notes, e0, e1, re0, re1, ri0, ri1, info0, info1, copies, sel):
    place = lax.axis_index("temp")
    lower = place != 0
    upper = place != lax.axis_size("temp") - 1
    n0, n1 = ri0[pl.ds(notes, 8), :], ri1[pl.ds(notes, 8), :]
    take0 = jnp.logical_and(n0[1:2, :] > 0.5, lower)
    take1 = jnp.logical_and(info0[1:2, :] > 0, upper)
    f0 = jnp.where(take0, re0[0:1, :], e0[0:1, :])
    f1 = jnp.where(take1, re1[0:1, :], e1[0:1, :])
    lane = lax.broadcasted_iota(jnp.int32, copies.shape, 1)
    shape = copies.shape
    copies[...] = jnp.where(
        lane == 0,
        jnp.broadcast_to(f0[:, : shape[1]], shape),
        jnp.broadcast_to(f1[:, : shape[1]], shape),
    )
    c0 = jnp.where(take0, n0[0:1, :], info0[0:1, :].astype(F32))
    c1 = jnp.where(take1, n1[0:1, :], info1[0:1, :].astype(F32))
    for i, v in enumerate((take0.astype(F32), take1.astype(F32), c0, c1)):
        sel[i] = (jnp.max(v) > 0.5).astype(jnp.int32)


def out_kernel(planes, half, *refs):
    sel, i0, i1, o0, o1, ri0, ri1, ro0, ro1, out_h, inner, outer, out, sems = refs
    core = core_index()
    columns = out.shape[-1]
    sources = (((i0, o0), (ri0, ro0)), ((i1, o1), (ri1, ro1)))

    def pull(slot, other):
        return [
            pltpu.make_async_copy(sources[slot][other][0], inner.at[slot], sems.at[slot]),
            pltpu.make_async_copy(sources[slot][other][1], outer.at[slot], sems.at[2 + slot]),
        ]

    for slot in range(2):
        for other in range(2):

            @pl.when(sel[slot] == other)
            def _():
                for copy in pull(slot, other):
                    copy.start()

    pushes = []
    for slot in range(2):
        for copy in pull(slot, 0):
            copy.wait()
        c = sel[2 + slot]
        a_of, b_of = inner.at[slot], outer.at[slot]
        for w in range(planes):
            z = w + core * (planes - 1 - 2 * w)
            m = lane_even(half, columns, w + c)
            for k in range(3):
                if 0 < w < planes - 1:
                    a = tile(a_of, 3 * (w - 1) + k, half)
                else:
                    a = tile(b_of, (0 if w == 0 else 3) + k, half)
                b = tile(b_of, 6 + 3 * w + k, half)
                out[slot, k, z, pl.ds(0, half, stride=2), :] = jnp.where(m, a, b)
                out[slot, k, z, pl.ds(1, half, stride=2), :] = jnp.where(m, b, a)
        push = pltpu.make_async_copy(out.at[slot], out_h.at[slot], sems.at[4 + slot])
        push.start()
        pushes.append(push)
    for push in pushes:
        push.wait()


def step(
    spin_state, couplings, inverse_temps, colour_order, heat_level, heat_height, heat_angle, swap_bits
):
    replicas, _, planes, rows, columns = spin_state.shape
    half = rows // 2
    assert replicas == 2 and planes == 4 and rows % 2 == 0 and columns % 2 == 0
    count = lax.axis_size("gz")
    temps = lax.axis_size("temp")
    in_chip = [(i, i ^ 1) for i in range(count)]
    cross = [(i, (i + (1 if i % 2 else -1)) % count) for i in range(count)]
    warmer = [(i, i + 1) for i in range(temps - 1)]
    colder = [(j, i) for i, j in warmer]

    def swap_in(value):
        return lax.ppermute(value, "gz", in_chip)

    def swap_cross(value):
        return lax.ppermute(value, "gz", cross)

    def away(value, slot):
        return lax.ppermute(value, "temp", warmer if slot else colder)

    spins = PIECES * half
    both = spins + 4 * rows
    p1x, p1i, p0x, p0i, am0, am1, info0, info1, beta0, beta1 = kernel_call(
        functools.partial(load_kernel, planes, half),
        [vm(both, columns)] * 2
        + [vm(spins, columns)] * 2
        + [vm(6 * half, columns)] * 2
        + [vm(8, columns, dtype=jnp.int32)] * 2
        + [vm(8, columns)] * 2,
        [HBM] * 5,
        scratch=[
            pltpu.SMEM((replicas,), jnp.int32),
            pltpu.SMEM((replicas,), jnp.int32),
            pltpu.SMEM((replicas,), F32),
            pltpu.VMEM(spin_state.shape, F32),
            pltpu.SemaphoreType.DMA((12,)),
        ],
    )(*(in_hbm(v) for v in (swap_bits, colour_order, inverse_temps, spin_state, couplings)))
    info, beta = [info0, info1], [beta0, beta1]
    sx, si, a_now = [p0x, p1x], [p0i, p1i], [am0, am1]
    rx1, ri1 = swap_cross(p1x), swap_in(p1i)
    rx0, ri0 = swap_cross(p0x), swap_in(p0i)
    rx, ri = [rx0, rx1], [ri0, ri1]

    ta0, tb0, ta1, tb1, dx, di = kernel_call(
        functools.partial(trial_kernel, planes, half),
        [vm(planes, 4, half, columns)] * 4 + [vm(6 * half, columns)] * 2,
        [SM, SM, VM, VM, VM],
    )(swap_bits, colour_order, heat_level, heat_height, heat_angle)
    trial_a, trial_b = [ta0, ta1], [tb0, tb1]
    rdx, rdi = swap_cross(dx), swap_in(di)

    weights = kernel_call(
        functools.partial(weight_kernel, planes, half),
        [vm(2, planes + 2, 6, half, columns)] * 2,
        [VM] * 5,
    )(couplings, rx1, ri1, info0, info1)

    for sweep in range(OR_SWEEPS):
        for slot in (1, 0):
            first = sweep == 0
            updated = vm(planes + 2, 3, half, columns)
            *a_next, sx[slot], si[slot] = kernel_call(
                functools.partial(relax_kernel, planes, half, first),
                [updated] * first + [vm(6 * half, columns)] * 2,
                [VM] * 7,
                scratch=[updated] * (not first),
            )(info[slot], weights[slot], sx[slot], si[slot], rx[slot], ri[slot], a_now[slot])
            a_now[slot] = a_next[0] if first else None
            rx[slot], ri[slot] = swap_cross(sx[slot]), swap_in(si[slot])

    inner, r_inner = [None] * 2, [None] * 2
    for slot in (1, 0):
        (inner[slot],) = kernel_call(
            functools.partial(inner_kernel, planes, half),
            [jax.ShapeDtypeStruct((3 * (planes - 2) * half + 8, columns), F32)],
            [VM] * 6,
        )(info[slot], beta[slot], weights[slot], sx[slot], si[slot], trial_a[slot])
        r_inner[slot] = away(inner[slot], slot)
    outer, r_outer, energy, r_energy = [None] * 2, [None] * 2, [None] * 2, [None] * 2
    for slot in (1, 0):
        outer[slot], energy[slot] = kernel_call(
            functools.partial(heat_kernel, planes, half, slot),
            [jax.ShapeDtypeStruct((18 * half, columns), F32), vm(8, columns)],
            [VM] * 12,
            scratch=[pltpu.VMEM((2, 3, half, columns), F32)],
        )(
            info[slot], beta[slot], weights[slot], sx[slot], si[slot], rx[slot], ri[slot],
            trial_a[slot], trial_b[slot], rdx, rdi, inner[slot],
        )
        r_energy[slot] = away(energy[slot], slot)
        r_outer[slot] = away(outer[slot], slot)
    r_inner, r_outer, r_energy = r_inner[::-1], r_outer[::-1], r_energy[::-1]

    copies, sel = kernel_call(
        functools.partial(decide_kernel, 3 * (planes - 2) * half),
        [vm(count, 2), jax.ShapeDtypeStruct((4,), jnp.int32)],
        [VM] * 8,
        out_specs=[VM, SM],
    )(energy[0], energy[1], r_energy[0], r_energy[1], r_inner[0], r_inner[1], info0, info1)
    parts = lax.all_to_all(copies, "gz", split_axis=0, concat_axis=0, tiled=True)
    energies = jnp.sum(parts, axis=0) / float(columns * rows * planes * count)

    (spin_final,) = kernel_call(
        functools.partial(out_kernel, planes, half),
        [jax.ShapeDtypeStruct(spin_state.shape, F32)],
        [SM] + [ANY] * 8,
        out_specs=[ANY],
        scratch=[
            pltpu.VMEM((2, *inner[0].shape), F32),
            pltpu.VMEM((2, *outer[0].shape), F32),
            pltpu.VMEM(spin_state.shape, F32),
            pltpu.SemaphoreType.DMA((6,)),
        ],
    )(sel, inner[0], inner[1], outer[0], outer[1], r_inner[0], r_inner[1], r_outer[0], r_outer[1])
    return spin_final, energies


def solution(mesh):
    return jax.shard_map(
        step,
        mesh=mesh,
        in_specs=(
            P(("group", "temp"), None, "gz", None, None),
            P(None, ("group", "gz"), None, None),
            P(("group", "temp")),
            P(("group", "temp")),
            P(("group", "temp"), "gz", None, None),
            P(("group", "temp"), "gz", None, None),
            P(("group", "temp"), "gz", None, None),
            P(("group", "temp")),
        ),
        out_specs=(P(("group", "temp"), None, "gz", None, None), P(("group", "temp"))),
        check_vma=False,
    )
```

profile of v0, /device:TPU:40, one launch (start us, length us, event | category | flops | bytes accessed | tf_op | source)
XLA Modules:
  0.0 97.4 jit_solution(9842983200442699935)
XLA Ops:
  0.6 1.7 %shard_map.95 = (f32[1088,128]{1,0:T(8,128)S(1)}, f32[1088,128]{1,0:T(8,128)S(1)}, f32[576,128]{1,0:T(8,128)S(1)}, f32[576,128]{1,0:T(8,128)S(1)}, f32[384,128]{...) custom-call(s32[2]{0:T(128)} %swap.1, s32[2]{0:T(128)} %colour.1, ...), custom_call_target="tpu_custom_call" | custom-call | tf_op jit(solution)/shard_map/pallas_call | solution.py:465
  2.4 22.0 %collective-permute-start = (f32[1088,128]{1,0:T(8,128)S(1)}, f32[1088,128]{1,0:T(8,128)S(1)}, u32[]{:S(2)}, u32[]{:S(2)}) collective-permute-start(f32[1088,128]{1,0:T(8,128)S(1)} %get-tuple-element.38.refs_2_), channel_id=1, source_target_pairs={{0,31},{1,2},{2,1},{3,4},{4,3},{5,6},{6,5},{7,8},{8,7},{9,10},{10,... | collective-permute-start | bytes 1671176 | tf_op jit(solution)/shard_map/ppermute | solution.py:458
  25.1 6.5 %collective-permute-done.rcx.refs_4_ = f32[1088,128]{1,0:T(8,128)S(1)} collective-permute-done((f32[1088,128]{1,0:T(8,128)S(1)}, f32[1088,128]{1,0:T(8,128)S(1)}, u32[]{:S(2)}, u32[]{:S(2)}) %collective-permute-start) | collective-permute-done | bytes 557088 | tf_op jit(solution)/shard_map/ppermute | solution.py:458
  32.0 1.1 %shard_map.102 = (f32[6,3,64,128]{3,2,1,0:T(8,128)S(1)}, f32[384,128]{1,0:T(8,128)S(1)}, f32[384,128]{1,0:T(8,128)S(1)}) custom-call(s32[8,128]{1,0:T(8,128)S(1)} %get-tuple-element.40.info1.refs_0_.info, f32[2,6,6,64,128]{4,3,2,1,0:T(8,128)S(1)} %get-tuple-element.56.refs_1_.weights.refs_2_, f32[1088,128]{1,0:T(8,128)S(1)} %get-tuple-element.38.refs_2_, ...), custom_call_target="tpu_custom_call" | custom-call | tf_op jit(solution)/shard_map/pallas_call | solution.py:505
  33.1 3.1 %collective-permute-start.10 = (f32[384,128]{1,0:T(8,128)S(1)}, f32[384,128]{1,0:T(8,128)S(1)}, u32[]{:S(2)}, u32[]{:S(2)}) collective-permute-start(f32[384,128]{1,0:T(8,128)S(1)} %get-tuple-element.58.refs_2_), channel_id=1, source_target_pairs={{0,31},{1,2},{2,1},{3,4},{4,3},{5,6},{6,5},{7,8},{8,7},{9,10},{10,... | collective-permute-start | bytes 589832 | tf_op jit(solution)/shard_map/ppermute | solution.py:458
  36.2 1.1 %shard_map.97 = (f32[6,3,64,128]{3,2,1,0:T(8,128)S(1)}, f32[384,128]{1,0:T(8,128)S(1)}, f32[384,128]{1,0:T(8,128)S(1)}) custom-call(s32[8,128]{1,0:T(8,128)S(1)} %get-tuple-element.36.info0.refs_0_.info, f32[2,6,6,64,128]{4,3,2,1,0:T(8,128)S(1)} %get-tuple-element.41.refs_1_.weights.refs_2_, f32[576,128]{1,0:T(8,128)S(1)} %get-tuple-element.42.refs_2_, ...), custom_call_target="tpu_custom_call" | custom-call | tf_op jit(solution)/shard_map/pallas_call | solution.py:505
  37.3 1.6 %collective-permute-start.4 = (f32[384,128]{1,0:T(8,128)S(1)}, f32[384,128]{1,0:T(8,128)S(1)}, u32[]{:S(2)}, u32[]{:S(2)}) collective-permute-start(f32[384,128]{1,0:T(8,128)S(1)} %get-tuple-element.45.refs_2_), channel_id=1, source_target_pairs={{0,31},{1,2},{2,1},{3,4},{4,3},{5,6},{6,5},{7,8},{8,7},{9,10},{10,... | collective-permute-start | bytes 589832 | tf_op jit(solution)/shard_map/ppermute | solution.py:458
  39.0 1.4 %shard_map.99 = (f32[4,4,64,128]{3,2,1,0:T(8,128)S(1)}, f32[4,4,64,128]{3,2,1,0:T(8,128)S(1)}, f32[4,4,64,128]{3,2,1,0:T(8,128)S(1)}, f32[4,4,64,128]{3,2,1,0:T(...) custom-call(s32[2]{0:T(128)S(1)} %copy-done.4, s32[2]{0:T(128)S(1)} %copy-done.5, ...), custom_call_target="tpu_custom_call" | custom-call | tf_op jit(solution)/shard_map/pallas_call | solution.py:487
  40.4 1.6 %collective-permute-start.8 = (f32[384,128]{1,0:T(8,128)S(1)}, f32[384,128]{1,0:T(8,128)S(1)}, u32[]{:S(2)}, u32[]{:S(2)}) collective-permute-start(f32[384,128]{1,0:T(8,128)S(1)} %get-tuple-element.52), channel_id=1, source_target_pairs={{0,31},{1,2},{2,1},{3,4},{4,3},{5,6},{6,5},{7,8},{8,7},{9,10},{10,... | collective-permute-start | bytes 589832 | tf_op jit(solution)/shard_map/ppermute | solution.py:458
  43.1 1.6 %collective-permute-start.12 = (f32[384,128]{1,0:T(8,128)S(1)}, f32[384,128]{1,0:T(8,128)S(1)}, u32[]{:S(2)}, u32[]{:S(2)}) collective-permute-start(f32[384,128]{1,0:T(8,128)S(1)} %get-tuple-element.61.sx.refs_3_), channel_id=1, source_target_pairs={{0,31},{1,2},{2,1},{3,4},{4,3},{5,6},{6,5},{7,8},{8,7},{9,10},{10,... | collective-permute-start | bytes 589832 | tf_op jit(solution)/shard_map/ppermute | solution.py:458
  45.8 1.6 %collective-permute-start.6 = (f32[384,128]{1,0:T(8,128)S(1)}, f32[384,128]{1,0:T(8,128)S(1)}, u32[]{:S(2)}, u32[]{:S(2)}) collective-permute-start(f32[384,128]{1,0:T(8,128)S(1)} %get-tuple-element.48.sx.refs_3_), channel_id=1, source_target_pairs={{0,31},{1,2},{2,1},{3,4},{4,3},{5,6},{6,5},{7,8},{8,7},{9,10},{10,... | collective-permute-start | bytes 589832 | tf_op jit(solution)/shard_map/ppermute | solution.py:458
  48.1 1.4 %collective-permute-done.12.refs_5_ = f32[384,128]{1,0:T(8,128)S(1)} collective-permute-done((f32[384,128]{1,0:T(8,128)S(1)}, f32[384,128]{1,0:T(8,128)S(1)}, u32[]{:S(2)}, u32[]{:S(2)}) %collective-permute-start.12) | collective-permute-done | bytes 196640 | tf_op jit(solution)/shard_map/ppermute | solution.py:458
  49.5 1.4 %shard_map.105 = (f32[1152,128]{1,0:T(8,128)S(1)}, f32[8,128]{1,0:T(8,128)S(1)}) custom-call(s32[8,128]{1,0:T(8,128)S(1)} %get-tuple-element.40.info1.refs_0_.info, f32[8,128]{1,0:T(8,128)S(1)} %get-tuple-element.55.betas.refs_1_, f32[2,6,6,64,128]{4,3,2,1,0:T(8,128)S(1)} %get-tuple-element.56.refs_1_.weights.refs_2_, ...), custom_call_target="tpu_custom_call" | custom-call | tf_op jit(solution)/shard_map/pallas_call | solution.py:524
  50.9 3.6 %collective-permute-start.18 = (f32[1152,128]{1,0:T(8,128)S(1)}, f32[1152,128]{1,0:T(8,128)S(1)}, u32[]{:S(2)}, u32[]{:S(2)}) collective-permute-start(f32[1152,128]{1,0:T(8,128)S(1)} %get-tuple-element.68.refs_4_), channel_id=1, source_target_pairs={{0,32},{32,64},{64,96},{1,33},{33,65},{65,97},{2,34},{34,66},{66,9... | collective-permute-start | bytes 1769480 | tf_op jit(solution)/shard_map/ppermute | solution.py:461
  54.5 1.4 %shard_map.101 = (f32[1152,128]{1,0:T(8,128)S(1)}, f32[8,128]{1,0:T(8,128)S(1)}) custom-call(s32[8,128]{1,0:T(8,128)S(1)} %get-tuple-element.36.info0.refs_0_.info, f32[8,128]{1,0:T(8,128)S(1)} %get-tuple-element.37.betas.refs_1_, f32[2,6,6,64,128]{4,3,2,1,0:T(8,128)S(1)} %get-tuple-element.41.refs_1_.weights.refs_2_, ...), custom_call_target="tpu_custom_call" | custom-call | tf_op jit(solution)/shard_map/pallas_call | solution.py:524
  55.9 1.3 %collective-permute-start.19 = (f32[1152,128]{1,0:T(8,128)S(1)}, f32[1152,128]{1,0:T(8,128)S(1)}, u32[]{:S(2)}, u32[]{:S(2)}) collective-permute-start(f32[1152,128]{1,0:T(8,128)S(1)} %get-tuple-element.67.refs_3_), channel_id=1, source_target_pairs={{32,0},{64,32},{96,64},{33,1},{65,33},{97,65},{34,2},{66,34},{98,6... | collective-permute-start | bytes 1769480 | tf_op jit(solution)/shard_map/ppermute | solution.py:461
  57.2 4.6 %collective-permute-start.16 = (f32[392,128]{1,0:T(8,128)S(1)}, f32[392,128]{1,0:T(8,128)S(1)}, u32[]{:S(2)}, u32[]{:S(2)}) collective-permute-start(f32[392,128]{1,0:T(8,128)S(1)} %shard_map.104.refs_11_.refs_2_), channel_id=1, source_target_pairs={{0,32},{32,64},{64,96},{1,33},{33,65},{65,97},{2,34},{34,66},{66,9... | collective-permute-start | bytes 602120 | tf_op jit(solution)/shard_map/ppermute | solution.py:461
  61.8 1.3 %collective-permute-start.17 = (f32[392,128]{1,0:T(8,128)S(1)}, f32[392,128]{1,0:T(8,128)S(1)}, u32[]{:S(2)}, u32[]{:S(2)}) collective-permute-start(f32[392,128]{1,0:T(8,128)S(1)} %shard_map.100.refs_11_.refs_1_), channel_id=1, source_target_pairs={{32,0},{64,32},{96,64},{33,1},{65,33},{97,65},{34,2},{66,34},{98,6... | collective-permute-start | bytes 602120 | tf_op jit(solution)/shard_map/ppermute | solution.py:461
  63.1 4.6 %collective-permute-start.14 = (f32[8,128]{1,0:T(8,128)S(1)}, f32[8,128]{1,0:T(8,128)S(1)}, u32[]{:S(2)}, u32[]{:S(2)}) collective-permute-start(f32[8,128]{1,0:T(8,128)S(1)} %get-tuple-element.65.e1), channel_id=1, source_target_pairs={{0,32},{32,64},{64,96},{1,33},{33,65},{65,97},{2,34},{34,66},{66,9... | collective-permute-start | bytes 12296 | tf_op jit(solution)/shard_map/ppermute | solution.py:461
  67.7 3.4 %collective-permute-done.14.re0 = f32[8,128]{1,0:T(8,128)S(1)} collective-permute-done((f32[8,128]{1,0:T(8,128)S(1)}, f32[8,128]{1,0:T(8,128)S(1)}, u32[]{:S(2)}, u32[]{:S(2)}) %collective-permute-start.14) | collective-permute-done | bytes 4128 | tf_op jit(solution)/shard_map/ppermute | solution.py:461
  71.1 1.3 %collective-permute-start.15 = (f32[8,128]{1,0:T(8,128)S(1)}, f32[8,128]{1,0:T(8,128)S(1)}, u32[]{:S(2)}, u32[]{:S(2)}) collective-permute-start(f32[8,128]{1,0:T(8,128)S(1)} %get-tuple-element.54.e0), channel_id=1, source_target_pairs={{32,0},{64,32},{96,64},{33,1},{65,33},{97,65},{34,2},{66,34},{98,6... | collective-permute-start | bytes 12296 | tf_op jit(solution)/shard_map/ppermute | solution.py:461
  72.5 4.7 %collective-permute-done.15.re1 = f32[8,128]{1,0:T(8,128)S(1)} collective-permute-done((f32[8,128]{1,0:T(8,128)S(1)}, f32[8,128]{1,0:T(8,128)S(1)}, u32[]{:S(2)}, u32[]{:S(2)}) %collective-permute-start.15) | collective-permute-done | bytes 4128 | tf_op jit(solution)/shard_map/ppermute | solution.py:461
  77.9 16.3 %all_to_all.9 = f32[32,1,2]{2,1,0:T(1,128)S(1)} all-to-all(f32[32,1,2]{2,1,0:T(1,128)S(1)} %bitcast.3), channel_id=1, replica_groups=mesh['group'=2,'temp'=4,'gz'=32] {'gz'}, dimensions={0} | all-to-all | bytes 512 | tf_op jit(solution)/shard_map/all_to_all | solution.py:543
  94.7 2.6 %shard_map.107 = f32[2,3,4,128,128]{4,3,2,1,0:T(8,128)} custom-call(s32[4]{0:T(128)S(1)} %get-tuple-element.66.refs_0_, f32[392,128]{1,0:T(8,128)S(1)} %shard_map.100.refs_11_.refs_1_, f32[392,128]{1,0:T(8,128)S(1)} %shard_map.104.refs_11_.refs_2_, f32[1152,128]{1,0:T(8,128)S(1)} %get-tuple-element.67.refs_3_, f32[1152,128]{1,0:T(8,128)S(1)} %get-tuple-element.68.refs_4_, ...), custom_call_target="tpu_custom_call" | custom-call | tf_op jit(solution)/shard_map/pallas_call | solution.py:546
  (44 shorter events, 5.4 us)
Async XLA Ops:
  0.6 31.0 %copy-start = (f32[3,4,128,128]{3,2,1,0:T(8,128)S(1)}, f32[3,4,128,128]{3,2,1,0:T(8,128)}, u32[]{:S(2)}) copy-start(f32[3,4,128,128]{3,2,1,0:T(8,128)} %coup.1) | copy-start | bytes 2359300
  2.4 29.2 %collective-permute-start = (f32[1088,128]{1,0:T(8,128)S(1)}, f32[1088,128]{1,0:T(8,128)S(1)}, u32[]{:S(2)}, u32[]{:S(2)}) collective-permute-start(f32[1088,128]{1,0:T(8,128)S(1)} %get-tuple-element.38.refs_2_), channel_id=1, source_target_pairs={{0,31},{1,2},{2,1},{3,4},{4,3},{5,6},{6,5},{7,8},{8,7},{9,10},{10,... | collective-permute-start | bytes 1671176 | tf_op jit(solution)/shard_map/ppermute | solution.py:458
  24.4 7.2 %collective-permute-start.1 = (f32[1088,128]{1,0:T(8,128)S(1)}, f32[1088,128]{1,0:T(8,128)S(1)}, u32[]{:S(2)}, u32[]{:S(2)}) collective-permute-start(f32[1088,128]{1,0:T(8,128)S(1)} %get-tuple-element.39.refs_3_), channel_id=1, source_target_pairs={{0,1},{1,0},{2,3},{3,2},{4,5},{5,4},{6,7},{7,6},{8,9},{9,8},{10,11... | collective-permute-start | bytes 1671176 | tf_op jit(solution)/shard_map/ppermute | solution.py:455
  24.4 11.8 %collective-permute-start.2 = (f32[576,128]{1,0:T(8,128)S(1)}, f32[576,128]{1,0:T(8,128)S(1)}, u32[]{:S(2)}, u32[]{:S(2)}) collective-permute-start(f32[576,128]{1,0:T(8,128)S(1)} %get-tuple-element.42.refs_2_), channel_id=1, source_target_pairs={{0,31},{1,2},{2,1},{3,4},{4,3},{5,6},{6,5},{7,8},{8,7},{9,10},{10,... | collective-permute-start | bytes 884744 | tf_op jit(solution)/shard_map/ppermute | solution.py:458
  25.1 11.1 %collective-permute-start.3 = (f32[576,128]{1,0:T(8,128)S(1)}, f32[576,128]{1,0:T(8,128)S(1)}, u32[]{:S(2)}, u32[]{:S(2)}) collective-permute-start(f32[576,128]{1,0:T(8,128)S(1)} %get-tuple-element.43.refs_3_), channel_id=1, source_target_pairs={{0,1},{1,0},{2,3},{3,2},{4,5},{5,4},{6,7},{7,6},{8,9},{9,8},{10,11... | collective-permute-start | bytes 884744 | tf_op jit(solution)/shard_map/ppermute | solution.py:455
  33.1 5.9 %copy-start.1 = (f32[2,4,128,128]{3,2,1,0:T(8,128)S(1)}, f32[2,4,128,128]{3,2,1,0:T(8,128)}, u32[]{:S(2)}) copy-start(f32[2,4,128,128]{3,2,1,0:T(8,128)} %level.1) | copy-start | bytes 1572868
  33.1 5.8 %copy-start.2 = (f32[2,4,128,128]{3,2,1,0:T(8,128)S(1)}, f32[2,4,128,128]{3,2,1,0:T(8,128)}, u32[]{:S(2)}) copy-start(f32[2,4,128,128]{3,2,1,0:T(8,128)} %height.1) | copy-start | bytes 1572868
  33.1 5.8 %copy-start.3 = (f32[2,4,128,128]{3,2,1,0:T(8,128)S(1)}, f32[2,4,128,128]{3,2,1,0:T(8,128)}, u32[]{:S(2)}) copy-start(f32[2,4,128,128]{3,2,1,0:T(8,128)} %angle.1) | copy-start | bytes 1572868
  33.1 8.8 %collective-permute-start.10 = (f32[384,128]{1,0:T(8,128)S(1)}, f32[384,128]{1,0:T(8,128)S(1)}, u32[]{:S(2)}, u32[]{:S(2)}) collective-permute-start(f32[384,128]{1,0:T(8,128)S(1)} %get-tuple-element.58.refs_2_), channel_id=1, source_target_pairs={{0,31},{1,2},{2,1},{3,4},{4,3},{5,6},{6,5},{7,8},{8,7},{9,10},{10,... | collective-permute-start | bytes 589832 | tf_op jit(solution)/shard_map/ppermute | solution.py:458
  36.2 5.8 %collective-permute-start.11 = (f32[384,128]{1,0:T(8,128)S(1)}, f32[384,128]{1,0:T(8,128)S(1)}, u32[]{:S(2)}, u32[]{:S(2)}) collective-permute-start(f32[384,128]{1,0:T(8,128)S(1)} %get-tuple-element.59.refs_3_), channel_id=1, source_target_pairs={{0,1},{1,0},{2,3},{3,2},{4,5},{5,4},{6,7},{7,6},{8,9},{9,8},{10,11... | collective-permute-start | bytes 589832 | tf_op jit(solution)/shard_map/ppermute | solution.py:455
  37.3 7.4 %collective-permute-start.4 = (f32[384,128]{1,0:T(8,128)S(1)}, f32[384,128]{1,0:T(8,128)S(1)}, u32[]{:S(2)}, u32[]{:S(2)}) collective-permute-start(f32[384,128]{1,0:T(8,128)S(1)} %get-tuple-element.45.refs_2_), channel_id=1, source_target_pairs={{0,31},{1,2},{2,1},{3,4},{4,3},{5,6},{6,5},{7,8},{8,7},{9,10},{10,... | collective-permute-start | bytes 589832 | tf_op jit(solution)/shard_map/ppermute | solution.py:458
  38.9 5.8 %collective-permute-start.5 = (f32[384,128]{1,0:T(8,128)S(1)}, f32[384,128]{1,0:T(8,128)S(1)}, u32[]{:S(2)}, u32[]{:S(2)}) collective-permute-start(f32[384,128]{1,0:T(8,128)S(1)} %get-tuple-element.46.refs_3_), channel_id=1, source_target_pairs={{0,1},{1,0},{2,3},{3,2},{4,5},{5,4},{6,7},{7,6},{8,9},{9,8},{10,11... | collective-permute-start | bytes 589832 | tf_op jit(solution)/shard_map/ppermute | solution.py:455
  40.4 7.0 %collective-permute-start.8 = (f32[384,128]{1,0:T(8,128)S(1)}, f32[384,128]{1,0:T(8,128)S(1)}, u32[]{:S(2)}, u32[]{:S(2)}) collective-permute-start(f32[384,128]{1,0:T(8,128)S(1)} %get-tuple-element.52), channel_id=1, source_target_pairs={{0,31},{1,2},{2,1},{3,4},{4,3},{5,6},{6,5},{7,8},{8,7},{9,10},{10,... | collective-permute-start | bytes 589832 | tf_op jit(solution)/shard_map/ppermute | solution.py:458
  42.0 6.1 %collective-permute-start.9 = (f32[384,128]{1,0:T(8,128)S(1)}, f32[384,128]{1,0:T(8,128)S(1)}, u32[]{:S(2)}, u32[]{:S(2)}) collective-permute-start(f32[384,128]{1,0:T(8,128)S(1)} %get-tuple-element.53), channel_id=1, source_target_pairs={{0,1},{1,0},{2,3},{3,2},{4,5},{5,4},{6,7},{7,6},{8,9},{9,8},{10,11... | collective-permute-start | bytes 589832 | tf_op jit(solution)/shard_map/ppermute | solution.py:455
  43.1 6.4 %collective-permute-start.12 = (f32[384,128]{1,0:T(8,128)S(1)}, f32[384,128]{1,0:T(8,128)S(1)}, u32[]{:S(2)}, u32[]{:S(2)}) collective-permute-start(f32[384,128]{1,0:T(8,128)S(1)} %get-tuple-element.61.sx.refs_3_), channel_id=1, source_target_pairs={{0,31},{1,2},{2,1},{3,4},{4,3},{5,6},{6,5},{7,8},{8,7},{9,10},{10,... | collective-permute-start | bytes 589832 | tf_op jit(solution)/shard_map/ppermute | solution.py:458
  44.7 4.8 %collective-permute-start.13 = (f32[384,128]{1,0:T(8,128)S(1)}, f32[384,128]{1,0:T(8,128)S(1)}, u32[]{:S(2)}, u32[]{:S(2)}) collective-permute-start(f32[384,128]{1,0:T(8,128)S(1)} %get-tuple-element.62.si.refs_4_), channel_id=1, source_target_pairs={{0,1},{1,0},{2,3},{3,2},{4,5},{5,4},{6,7},{7,6},{8,9},{9,8},{10,11... | collective-permute-start | bytes 589832 | tf_op jit(solution)/shard_map/ppermute | solution.py:455
  45.8 8.7 %collective-permute-start.6 = (f32[384,128]{1,0:T(8,128)S(1)}, f32[384,128]{1,0:T(8,128)S(1)}, u32[]{:S(2)}, u32[]{:S(2)}) collective-permute-start(f32[384,128]{1,0:T(8,128)S(1)} %get-tuple-element.48.sx.refs_3_), channel_id=1, source_target_pairs={{0,31},{1,2},{2,1},{3,4},{4,3},{5,6},{6,5},{7,8},{8,7},{9,10},{10,... | collective-permute-start | bytes 589832 | tf_op jit(solution)/shard_map/ppermute | solution.py:458
  47.3 7.1 %collective-permute-start.7 = (f32[384,128]{1,0:T(8,128)S(1)}, f32[384,128]{1,0:T(8,128)S(1)}, u32[]{:S(2)}, u32[]{:S(2)}) collective-permute-start(f32[384,128]{1,0:T(8,128)S(1)} %get-tuple-element.49.si.refs_4_), channel_id=1, source_target_pairs={{0,1},{1,0},{2,3},{3,2},{4,5},{5,4},{6,7},{7,6},{8,9},{9,8},{10,11... | collective-permute-start | bytes 589832 | tf_op jit(solution)/shard_map/ppermute | solution.py:455
  50.9 43.8 %collective-permute-start.18 = (f32[1152,128]{1,0:T(8,128)S(1)}, f32[1152,128]{1,0:T(8,128)S(1)}, u32[]{:S(2)}, u32[]{:S(2)}) collective-permute-start(f32[1152,128]{1,0:T(8,128)S(1)} %get-tuple-element.68.refs_4_), channel_id=1, source_target_pairs={{0,32},{32,64},{64,96},{1,33},{33,65},{65,97},{2,34},{34,66},{66,9... | collective-permute-start | bytes 1769480 | tf_op jit(solution)/shard_map/ppermute | solution.py:461
  55.9 38.8 %collective-permute-start.19 = (f32[1152,128]{1,0:T(8,128)S(1)}, f32[1152,128]{1,0:T(8,128)S(1)}, u32[]{:S(2)}, u32[]{:S(2)}) collective-permute-start(f32[1152,128]{1,0:T(8,128)S(1)} %get-tuple-element.67.refs_3_), channel_id=1, source_target_pairs={{32,0},{64,32},{96,64},{33,1},{65,33},{97,65},{34,2},{66,34},{98,6... | collective-permute-start | bytes 1769480 | tf_op jit(solution)/shard_map/ppermute | solution.py:461
  57.2 15.2 %collective-permute-start.16 = (f32[392,128]{1,0:T(8,128)S(1)}, f32[392,128]{1,0:T(8,128)S(1)}, u32[]{:S(2)}, u32[]{:S(2)}) collective-permute-start(f32[392,128]{1,0:T(8,128)S(1)} %shard_map.104.refs_11_.refs_2_), channel_id=1, source_target_pairs={{0,32},{32,64},{64,96},{1,33},{33,65},{65,97},{2,34},{34,66},{66,9... | collective-permute-start | bytes 602120 | tf_op jit(solution)/shard_map/ppermute | solution.py:461
  61.8 15.3 %collective-permute-start.17 = (f32[392,128]{1,0:T(8,128)S(1)}, f32[392,128]{1,0:T(8,128)S(1)}, u32[]{:S(2)}, u32[]{:S(2)}) collective-permute-start(f32[392,128]{1,0:T(8,128)S(1)} %shard_map.100.refs_11_.refs_1_), channel_id=1, source_target_pairs={{32,0},{64,32},{96,64},{33,1},{65,33},{97,65},{34,2},{66,34},{98,6... | collective-permute-start | bytes 602120 | tf_op jit(solution)/shard_map/ppermute | solution.py:461
  63.1 8.0 %collective-permute-start.14 = (f32[8,128]{1,0:T(8,128)S(1)}, f32[8,128]{1,0:T(8,128)S(1)}, u32[]{:S(2)}, u32[]{:S(2)}) collective-permute-start(f32[8,128]{1,0:T(8,128)S(1)} %get-tuple-element.65.e1), channel_id=1, source_target_pairs={{0,32},{32,64},{64,96},{1,33},{33,65},{65,97},{2,34},{34,66},{66,9... | collective-permute-start | bytes 12296 | tf_op jit(solution)/shard_map/ppermute | solution.py:461
  71.1 6.0 %collective-permute-start.15 = (f32[8,128]{1,0:T(8,128)S(1)}, f32[8,128]{1,0:T(8,128)S(1)}, u32[]{:S(2)}, u32[]{:S(2)}) collective-permute-start(f32[8,128]{1,0:T(8,128)S(1)} %get-tuple-element.54.e0), channel_id=1, source_target_pairs={{32,0},{64,32},{96,64},{33,1},{65,33},{97,65},{34,2},{66,34},{98,6... | collective-permute-start | bytes 12296 | tf_op jit(solution)/shard_map/ppermute | solution.py:461
  (2 other events, 11.7 us)
where the time goes:
time: 98.2 us; the launch traced here: 97.4 us
  starting transfers between devices  48.9 us (50%)
  blocking collectives  16.3 us (17%)
  waiting for transfers between devices  16 us (16%)
  Pallas kernels  14.6 us (15%)
  between operations  1.04 us (1%)
    ppermute x7, starting transfers between devices, swap_cross(): return lax.ppermute(value, 'gz', cross)  32.2 us
    ppermute x6, starting transfers between devices, away(): return lax.ppermute(value, 'temp', warmer if slot else colder)  16.7 us
    all_to_all x1, blocking collectives, step(): lax.all_to_all(copies, 'gz', split_axis=0, concat_axis=0, tiled=True)  16.3 us
    ppermute x6, waiting for transfers between devices, away(): return lax.ppermute(value, 'temp', warmer if slot else colder)  8.08 us
    ppermute x7, waiting for transfers between devices, swap_cross(): return lax.ppermute(value, 'gz', cross)  7.87 us
    pallas_call x4, Pallas kernels, step(): kernel_call(functools.partial(relax_kernel, planes, half, first), [update...  4.3 us
    pallas_call x2, Pallas kernels, step(): kernel_call(functools.partial(heat_kernel, planes, half, slot), [jax.Shap...  2.78 us
    pallas_call x1, Pallas kernels, step(): kernel_call(functools.partial(out_kernel, planes, half), [jax.ShapeDtypeS...  2.58 us
  transfers between devices with their start and end apart: 20, of which 4 were waited for; matrix products, arithmetic and copies ran while one was open for 1% of the time, Pallas kernels for 11%

commit v1 on v0

v1 whole, which is shorter than its diff:
```python
import functools

import jax
import jax.numpy as jnp
from jax import lax
from jax.experimental import pallas as pl
from jax.experimental.pallas import tpu as pltpu
from jax.sharding import PartitionSpec as P


F32 = jnp.float32
OR_SWEEPS = 2


VM = pl.BlockSpec(memory_space=pltpu.VMEM)
SM = pl.BlockSpec(memory_space=pltpu.SMEM)
ANY = pl.BlockSpec(memory_space=pl.ANY)
HBM = pl.BlockSpec(memory_space=pltpu.HBM)
PIECES = 9
EARLY = 15
LATE = 9


def vm(*shape, dtype=F32):
    return pltpu.VMEM(shape, dtype)


def kernel_call(body, outs, in_specs, out_specs=None, scratch=(), mib=24):
    return pl.pallas_call(
        body,
        out_shape=outs,
        in_specs=in_specs,
        out_specs=out_specs if out_specs is not None else [VM] * len(outs),
        scratch_shapes=list(scratch),
        compiler_params=pltpu.CompilerParams(vmem_limit_bytes=mib * 1024 * 1024),
    )


def in_hbm(value):
    return pltpu.with_memory_space_constraint(value, pltpu.HBM)


def core_index():
    return lax.rem(lax.axis_index("gz"), 2)


def slot_of(u):
    odd = lax.rem(lax.axis_index("temp"), 2)
    return 1 - odd if u == 0 else odd


def slot_replica(swap, u):
    return slot_of(u) ^ (swap[0] != 0).astype(jnp.int32)


def lane_even(rows, columns, offset):
    lane = lax.broadcasted_iota(jnp.int32, (rows, columns), 1)
    return ((lane + offset) & 1) == 0


def tile(ref, i, half):
    return ref[pl.ds(i * half, half), :]


def put(ref, i, value):
    half = value.shape[0]
    ref[pl.ds(i * half, half), :] = value


def folded(ref, index, half):
    return tuple(ref[(*index, pl.ds(s, half, stride=2), slice(None))] for s in (0, 1))


def folded_rows(ref, base, half):
    return tuple(ref[pl.ds(base + s, half, stride=2), :] for s in (0, 1))


def parity(info, half):
    columns = info.shape[-1]
    lane = lax.broadcasted_iota(jnp.int32, (half, columns), 1)
    return (lane & 1) == jnp.broadcast_to(info[0:1, :], (half, columns))


def at_plane(even, w):
    return even if w % 2 == 0 else jnp.logical_not(even)


def load_kernel(planes, half, *refs):
    (swap_h, colour_h, beta_h, spin_h, coup_h) = refs[:5]
    (p0x, p0i, p1x, p1i, am0, am1, info0, info1, beta0, beta1) = refs[5:15]
    swap, colour, betas, spin, sems = refs[15:]
    core = core_index()
    columns = spin.shape[-1]
    rows = 2 * half
    top = planes - 1
    scalars = [
        pltpu.make_async_copy(swap_h, swap, sems.at[0]),
        pltpu.make_async_copy(colour_h, colour, sems.at[1]),
        pltpu.make_async_copy(beta_h, betas, sems.at[2]),
    ]
    spins = [
        pltpu.make_async_copy(spin_h.at[:, :, w + core * (top - 2 * w)], spin.at[w], sems.at[3 + w])
        for w in range(planes)
    ]
    bonds = []
    zx = core * top
    zi = top - zx
    for ref, z, near, outer, sem in (
        (p0x, zx, core * (top - 1), zx, 3 + planes),
        (p0i, zi, (1 - core) * (top - 1), zi, 7 + planes),
    ):
        for i, (d, p) in enumerate(((0, z), (1, z), (2, near), (2, outer))):
            target = ref.at[pl.ds(PIECES * half + i * rows, rows), :]
            bonds.append(pltpu.make_async_copy(coup_h.at[d, p], target, sems.at[sem + i]))
    for copy in scalars + spins + bonds:
        copy.start()
    for copy in scalars:
        copy.wait()
    reps, masks = [], []
    for u, info, beta in ((0, info0, beta0), (1, info1, beta1)):
        rep = slot_replica(swap, u)
        c = colour[rep] ^ core
        info[0:1, :] = jnp.full((1, columns), c, jnp.int32)
        info[1:2, :] = jnp.full((1, columns), (swap[1] != 0).astype(jnp.int32), jnp.int32)
        beta[...] = jnp.full(beta.shape, betas[rep], F32)
        reps.append(rep)
        masks.append(lane_even(half, columns, c))
    for w in range(planes):
        spins[w].wait()
        for u, sx, si, am in ((0, p0x, p0i, am0), (1, p1x, p1i, am1)):
            m = at_plane(masks[u], w)
            for k in range(3):
                even, odd = folded(spin, (w, reps[u], k), half)
                a = jnp.where(m, even, odd)
                b = jnp.where(m, odd, even)
                if w == 0:
                    put(sx, k, b)
                    put(sx, 6 + k, a)
                elif w == 1:
                    put(sx, 3 + k, b)
                    put(am, k, a)
                elif w == planes - 2:
                    put(si, 3 + k, b)
                    put(am, 3 + k, a)
                else:
                    put(si, k, b)
                    put(si, 6 + k, a)
    for copy in bonds:
        copy.wait()


def weight_kernel(planes, half, in_chip, *refs):
    coup, sent_ref, info0, info1, weights0, weights1 = refs
    core = core_index()
    top = planes - 1
    rows = 2 * half
    first = core == 0

    def sent(i):
        return folded_rows(sent_ref, PIECES * half + i * rows, half)

    def zbond(m):
        if m in (-1, planes + 1):
            return sent(2)
        if m in (0, planes):
            ours, theirs = folded(coup, (2, top), half), sent(3)
            mine = first if m == planes else jnp.logical_not(first)
            return tuple(jnp.where(mine, o, t) for o, t in zip(ours, theirs))
        return folded(coup, (2, (m - 1) + core * (top - 2 * m + 1)), half)

    span = range(1, planes + 1) if in_chip else range(-1, 1)
    below = zbond(span[0])
    for i, w in enumerate(span):
        above = zbond(w + 1)
        if w in (-1, planes):
            jx, jy = sent(0), sent(1)
        else:
            z = w + core * (top - 2 * w)
            jx, jy = folded(coup, (0, z), half), folded(coup, (1, z), half)
        up_odd = pltpu.roll(jy[1], 1, 0)
        for info, weights in ((info0, weights0), (info1, weights1)):
            even = parity(info, half)
            for a in (0, 1):
                if a == 1 and w in (-1, planes):
                    continue
                m = at_plane(even, w + a)
                weights[a, i, 0] = jnp.where(m, jx[0], jx[1])
                weights[a, i, 1] = pltpu.roll(jnp.where(m, jx[1], jx[0]), 1, 1)
                weights[a, i, 2] = jy[0]
                weights[a, i, 3] = jnp.where(m, up_odd, jy[1])
                weights[a, i, 4] = jnp.where(m, above[0], above[1])
                weights[a, i, 5] = jnp.where(m, below[0], below[1])
        below = above


def field(get, weight, a, even, w):
    total = []
    m = at_plane(even, w + a)
    for k in range(3):
        o = get(w, k)
        half, columns = o.shape
        side = jnp.where(m, pltpu.roll(o, 1, 0), pltpu.roll(o, half - 1, 0))
        h = weight(a, w, 0) * pltpu.roll(o, columns - 1, 1)
        h = h + weight(a, w, 1) * pltpu.roll(o, 1, 1)
        h = h + weight(a, w, 2) * o
        h = h + weight(a, w, 3) * side
        h = h + weight(a, w, 4) * get(w + 1, k)
        h = h + weight(a, w, 5) * get(w - 1, k)
        total.append(h)
    return total


def weight_of(w_in, w_x):
    return lambda a, w, i: w_in[a, w - 1, i] if w > 0 else w_x[a, w + 1, i]


def dot3(a, b):
    return a[0] * b[0] + a[1] * b[1] + a[2] * b[2]


def reflect(s, h):
    f = 2.0 * dot3(s, h) / jnp.maximum(dot3(h, h), 0.01)
    return [f * h[k] - s[k] for k in range(3)]


def second_planes(planes, half, sx, si, rx, ri):
    def get(w, k):
        if w < 0:
            return tile(rx, 3 * (-1 - w) + k, half)
        if w < 2:
            return tile(sx, 3 * w + k, half)
        if w < planes:
            return tile(si, 3 * (planes - 1 - w) + k, half)
        return tile(ri, 3 * (w - planes) + k, half)

    return get


def relax_early(planes, half, first, *refs):
    info, w_in, sx, si, ri, a_old, a_new, bi = refs
    even = parity(info, half)
    weight = weight_of(w_in, None)
    get_b = second_planes(planes, half, sx, si, None, ri)

    def get_a(w, k):
        if not first:
            return tile(a_old, 3 * (w - 1) + k, half)
        if w == planes - 1:
            return tile(si, 6 + k, half)
        if w == planes:
            return tile(ri, 6 + k, half)
        return tile(a_old, 3 * (w - 1) + k, half)

    for w in range(1, planes + 1):
        h = field(get_b, weight, 0, even, w)
        new = reflect([get_a(w, k) for k in range(3)], h)
        for k in range(3):
            put(a_new, 3 * (w - 1) + k, new[k])
    for w in range(2, planes):
        h = field(lambda v, k: tile(a_new, 3 * (v - 1) + k, half), weight, 1, even, w)
        new = reflect([get_b(w, k) for k in range(3)], h)
        for k in range(3):
            put(bi, 3 * (planes - 1 - w) + k, new[k])


def relax_late(planes, half, first, *refs):
    info, w_in, w_x, sx, rx, a_in = refs[:6]
    a_old, a_new, bx = (None, *refs[6:]) if first else (refs[6], refs[8], refs[7])
    even = parity(info, half)
    weight = weight_of(w_in, w_x)
    get_b = second_planes(planes, half, sx, None, rx, None)

    def get_a(w, k):
        if not first:
            return tile(a_old, 3 * (w + 1) + k, half)
        return tile(rx if w < 0 else sx, 6 + k, half)

    for w in (-1, 0):
        h = field(get_b, weight, 0, even, w)
        new = reflect([get_a(w, k) for k in range(3)], h)
        for k in range(3):
            put(a_new, 3 * (w + 1) + k, new[k])

    def get_new(w, k):
        return tile(a_new, 3 * (w + 1) + k, half) if w < 1 else tile(a_in, 3 * (w - 1) + k, half)

    for w in (0, 1):
        h = field(get_new, weight, 1, even, w)
        new = reflect([get_b(w, k) for k in range(3)], h)
        for k in range(3):
            put(bx, 3 * w + k, new[k])


SIN = (1.0, -1 / 6, 1 / 120, -1 / 5040, 1 / 362880, -1 / 39916800, 1 / 6227020800)
COS = (1.0, -1 / 2, 1 / 24, -1 / 720, 1 / 40320, -1 / 3628800, 1 / 479001600, -1 / 87178291200)


def series(coefficients, y):
    total = coefficients[-1]
    for value in coefficients[-2::-1]:
        total = total * y + value
    return total


def trial(height, angle):
    t = 0.5 * angle
    y = t * t
    s = t * series(SIN, y)
    c = series(COS, y)
    q = jnp.sqrt(jnp.maximum(1.0 - height * height, 0.0))
    return q * (1.0 - 2.0 * (s * s)), q * (2.0 * (s * c))


def trial_kernel(planes, half, swap, colour, level, height, angle, ta0, tb0, ta1, tb1, dx, di):
    core = core_index()
    columns = level.shape[-1]
    for u, ta, tb in ((0, ta0, tb0), (1, ta1, tb1)):
        rep = slot_replica(swap, u)
        c = colour[rep]
        for w in range(planes):
            z = w + core * (planes - 1 - 2 * w)
            m = lane_even(half, columns, z + c)
            a, b = [], []
            for ref in (level, height, angle):
                even, odd = folded(ref, (rep, z), half)
                a.append(jnp.where(m, even, odd))
                b.append(jnp.where(m, odd, even))
            if w == 0 or w == planes - 1:
                for i in range(3):
                    put(dx if w == 0 else di, 3 * u + i, a[i])
            for t, (lev, hei, ang) in ((ta, a), (tb, b)):
                ux, uy = trial(hei, ang)
                t[w, 0], t[w, 1], t[w, 2], t[w, 3] = ux, uy, hei, lev


def trial_of(t, w):
    return [t[w, k] for k in range(3)], t[w, 3]


def trial_sent(draws, u, half):
    level, height, angle = (tile(draws, 3 * u + i, half) for i in range(3))
    ux, uy = trial(height, angle)
    return [ux, uy, height], level


def heated(h, u, level, beta):
    m = jnp.maximum(dot3(h, h), 0.01)
    inverse = lax.rsqrt(m)
    e = [h[k] * inverse for k in range(3)]
    reach = beta * (m * inverse)
    c = 1.0 + jnp.log(1.0 + level * (jnp.exp(-2.0 * reach) - 1.0)) / reach
    along = dot3(u, e)
    t = [u[k] - along * e[k] for k in range(3)]
    f = jnp.sqrt(jnp.maximum(1.0 - c * c, 0.0)) * lax.rsqrt(jnp.maximum(dot3(t, t), 0.0001))
    return [c * e[k] + f * t[k] for k in range(3)]


def heat_early(planes, half, u, *refs):
    info, betas, w_in, sx, si, ri, ta, tb, rdi, out, e_part, halo = refs
    even = parity(info, half)
    columns = info.shape[-1]
    beta = jnp.broadcast_to(betas[0:1, :], (half, columns))
    weight = weight_of(w_in, None)
    get_b = second_planes(planes, half, sx, si, None, ri)

    def get_a(w, k):
        return halo[k] if w == planes else tile(out, 3 * (w - 1) + k, half)

    for w in range(1, planes + 1):
        h = field(get_b, weight, 0, even, w)
        draw = trial_of(ta, w) if w < planes else trial_sent(rdi, u, half)
        new = heated(h, *draw, beta)
        for k in range(3):
            if w == planes:
                halo[k] = new[k]
            else:
                put(out, 3 * (w - 1) + k, new[k])
    energy = None
    for w in range(2, planes):
        h = field(get_a, weight, 1, even, w)
        new = heated(h, *trial_of(tb, w), beta)
        for k in range(3):
            put(out, 9 + 3 * (w - 2) + k, new[k])
        term = dot3(new, h)
        energy = term if energy is None else energy + term
    e_part[...] = energy
    out[pl.ds(EARLY * half, 8), :] = info[...].astype(F32)


def heat_late(planes, half, u, *refs):
    info, betas, w_in, w_x, sx, rx, ta, tb, rdx, inner, e_part = refs[:11]
    if u == 0:
        out, e_out, halo = refs[11:]
    else:
        e_other, out, e_out, halo = refs[11:]
    even = parity(info, half)
    columns = info.shape[-1]
    beta = jnp.broadcast_to(betas[0:1, :], (half, columns))
    weight = weight_of(w_in, w_x)
    get_b = second_planes(planes, half, sx, None, rx, None)

    def get_a(w, k):
        if w < 0:
            return halo[k]
        return tile(out, k, half) if w == 0 else tile(inner, 3 * (w - 1) + k, half)

    for w in (-1, 0):
        h = field(get_b, weight, 0, even, w)
        draw = trial_of(ta, w) if w >= 0 else trial_sent(rdx, u, half)
        new = heated(h, *draw, beta)
        for k in range(3):
            if w < 0:
                halo[k] = new[k]
            else:
                put(out, k, new[k])
    energy = e_part[...]
    for w in (0, 1):
        h = field(get_a, weight, 1, even, w)
        new = heated(h, *trial_of(tb, w), beta)
        for k in range(3):
            put(out, 3 + 3 * w + k, new[k])
        energy = energy + dot3(new, h)
    mine = jnp.full(e_out.shape, -jnp.sum(energy), F32)
    if u == 1:
        lane = lax.broadcasted_iota(jnp.int32, e_out.shape, 1)
        other = jnp.broadcast_to(e_other[0:1, : e_out.shape[1]], e_out.shape)
        mine = jnp.where(lane == 0, other, mine)
    e_out[...] = mine


def total_kernel(sites, parts, total):
    total[...] = jnp.sum(parts[...], axis=0, keepdims=True) / sites


def exchanged(u, info, note):
    place = lax.axis_index("temp")
    upper = slot_of(u) == 1
    ours = jnp.max(info[1:2, :]) > 0
    theirs = jnp.max(note[1:2, :]) > 0.5
    inside = jnp.where(upper, place != lax.axis_size("temp") - 1, place != 0)
    return jnp.logical_and(jnp.where(upper, ours, theirs), inside)


def out_kernel(planes, half, *refs):
    info0, info1, i0, i1, o0, o1, ri0, ri1, ro0, ro1, out_h, out, sems = refs
    core = core_index()
    columns = out.shape[-1]
    pushes = []
    for u, info, own, other in ((0, info0, (i0, o0), (ri0, ro0)), (1, info1, (i1, o1), (ri1, ro1))):
        note = ri0[pl.ds(EARLY * half, 8), :] if u == 0 else ri1[pl.ds(EARLY * half, 8), :]
        take = exchanged(u, info, note)

        def write(early, late, parities):
            even = (lax.broadcasted_iota(jnp.int32, (half, columns), 1) & 1) == jnp.broadcast_to(
                parities, (half, columns)
            )
            for w in range(planes):
                z = w + core * (planes - 1 - 2 * w)
                m = at_plane(even, w)
                for k in range(3):
                    a = tile(late, k, half) if w == 0 else tile(early, 3 * (w - 1) + k, half)
                    b = tile(late, 3 + 3 * w + k, half) if w < 2 else tile(early, 3 + 3 * w + k, half)
                    out[u, k, z, pl.ds(0, half, stride=2), :] = jnp.where(m, a, b)
                    out[u, k, z, pl.ds(1, half, stride=2), :] = jnp.where(m, b, a)

        @pl.when(take)
        def _():
            write(*other, note[0:1, :].astype(jnp.int32))

        @pl.when(jnp.logical_not(take))
        def _():
            write(*own, info[0:1, :])

        push = pltpu.make_async_copy(out.at[u], out_h.at[slot_of(u)], sems.at[u])
        push.start()
        pushes.append(push)
    for push in pushes:
        push.wait()


def energy_kernel(half, info0, info1, total, r0, r1, ri0, ri1, energies):
    final = []
    for u, info, r, ri in ((0, info0, r0, ri0), (1, info1, r1, ri1)):
        take = exchanged(u, info, ri[pl.ds(EARLY * half, 8), :])
        final.append(jnp.where(take, r[...], total[...]))
    lane = lax.broadcasted_iota(jnp.int32, energies.shape, 1)
    sums = [jnp.sum(jnp.where(lane == u, final[u], 0.0)) for u in range(2)]
    energies[...] = jnp.where(lane == slot_of(0), sums[0], sums[1])


def step(
    spin_state, couplings, inverse_temps, colour_order, heat_level, heat_height, heat_angle, swap_bits
):
    replicas, _, planes, rows, columns = spin_state.shape
    half = rows // 2
    count = lax.axis_size("gz")
    temps = lax.axis_size("temp")
    assert replicas == 2 and planes == 4 and rows % 2 == 0 and columns % 2 == 0
    assert count % 2 == 0 and temps % 2 == 0
    in_chip = [(i, i ^ 1) for i in range(count)]
    cross = [(i, (i + (1 if i % 2 else -1)) % count) for i in range(count)]
    partners = (
        [(i, i ^ 1) for i in range(temps)],
        [(i, (i + (1 if i % 2 else -1)) % temps) for i in range(temps)],
    )

    def swap_in(value):
        return lax.ppermute(value, "gz", in_chip)

    def swap_cross(value):
        return lax.ppermute(value, "gz", cross)

    def away(value, u):
        return lax.ppermute(value, "temp", partners[u])

    spins = PIECES * half
    both = spins + 4 * rows
    pair = vm(6 * half, columns)
    p0x, p0i, p1x, p1i, am0, am1, info0, info1, beta0, beta1 = kernel_call(
        functools.partial(load_kernel, planes, half),
        [vm(both, columns)] * 2
        + [vm(spins, columns)] * 2
        + [pair] * 2
        + [vm(8, columns, dtype=jnp.int32)] * 2
        + [vm(8, columns)] * 2,
        [HBM] * 5,
        scratch=[
            pltpu.SMEM((replicas,), jnp.int32),
            pltpu.SMEM((replicas,), jnp.int32),
            pltpu.SMEM((replicas,), F32),
            vm(planes, replicas, 3, rows, columns),
            pltpu.SemaphoreType.DMA((11 + planes,)),
        ],
    )(*(in_hbm(v) for v in (swap_bits, colour_order, inverse_temps, spin_state, couplings)))
    info, beta = [info0, info1], [beta0, beta1]
    sx, si, a_in, a_x = [p0x, p1x], [p0i, p1i], [am0, am1], [[], []]
    rx = [swap_cross(sx[u]) for u in range(2)]
    ri = [swap_in(si[u]) for u in range(2)]

    ta0, tb0, ta1, tb1, dx, di = kernel_call(
        functools.partial(trial_kernel, planes, half),
        [vm(planes, 4, half, columns)] * 4 + [pair] * 2,
        [SM, SM, VM, VM, VM],
    )(swap_bits, colour_order, heat_level, heat_height, heat_angle)
    trial_a, trial_b = [ta0, ta1], [tb0, tb1]
    rdx, rdi = swap_cross(dx), swap_in(di)

    w_in = kernel_call(
        functools.partial(weight_kernel, planes, half, True),
        [vm(2, planes, 6, half, columns)] * 2,
        [VM] * 4,
    )(couplings, ri[0], info0, info1)
    w_x = kernel_call(
        functools.partial(weight_kernel, planes, half, False),
        [vm(2, 2, 6, half, columns)] * 2,
        [VM] * 4,
    )(couplings, rx[0], info0, info1)

    assert OR_SWEEPS == 2
    for sweep in range(OR_SWEEPS):
        first = sweep == 0
        new_in, bi = [None] * 2, [None] * 2
        for u in range(2):
            new_in[u], bi[u] = kernel_call(
                functools.partial(relax_early, planes, half, first),
                [vm(3 * planes * half, columns), pair],
                [VM] * 6,
            )(info[u], w_in[u], sx[u], si[u], ri[u], a_in[u])
        for u in range(2):
            *a_x[u], sx[u] = kernel_call(
                functools.partial(relax_late, planes, half, first),
                [pair] * (1 + first),
                [VM] * (6 if first else 7),
                scratch=[] if first else [pair],
            )(info[u], w_in[u], w_x[u], sx[u], rx[u], new_in[u], *a_x[u])
            si[u], a_in[u] = bi[u], new_in[u]
            rx[u] = swap_cross(sx[u])
            ri[u] = swap_in(si[u])

    inner, outer, part, r_inner, r_outer = ([None] * 2 for _ in range(5))
    for u in range(2):
        inner[u], part[u] = kernel_call(
            functools.partial(heat_early, planes, half, u),
            [vm(EARLY * half + 8, columns), vm(half, columns)],
            [VM] * 9,
            scratch=[vm(3, half, columns)],
        )(info[u], beta[u], w_in[u], sx[u], si[u], ri[u], trial_a[u], trial_b[u], rdi)
        r_inner[u] = away(inner[u], u)
    energy = []
    for u in range(2):
        outer[u], *energy = kernel_call(
            functools.partial(heat_late, planes, half, u),
            [vm(LATE * half, columns), vm(count, 2) if u else vm(8, columns)],
            [VM] * (11 + u),
            scratch=[vm(3, half, columns)],
        )(
            info[u], beta[u], w_in[u], w_x[u], sx[u], rx[u],
            trial_a[u], trial_b[u], rdx, inner[u], part[u], *energy,
        )
        r_outer[u] = away(outer[u], u)

    parts = lax.all_to_all(energy[0], "gz", split_axis=0, concat_axis=0, tiled=True)
    (total,) = kernel_call(
        functools.partial(total_kernel, float(columns * rows * planes * count)), [vm(1, 2)], [VM]
    )(parts)
    r_total = [away(total, u) for u in range(2)]

    (spin_final,) = kernel_call(
        functools.partial(out_kernel, planes, half),
        [jax.ShapeDtypeStruct(spin_state.shape, F32)],
        [VM] * 10,
        out_specs=[ANY],
        scratch=[vm(*spin_state.shape), pltpu.SemaphoreType.DMA((2,))],
    )(info0, info1, *inner, *outer, *r_inner, *r_outer)
    (energies,) = kernel_call(
        functools.partial(energy_kernel, half), [vm(1, 2)], [VM] * 7
    )(info0, info1, total, *r_total, *r_inner)
    return spin_final, energies.reshape(-1)


def solution(mesh):
    return jax.shard_map(
        step,
        mesh=mesh,
        in_specs=(
            P(("group", "temp"), None, "gz", None, None),
            P(None, ("group", "gz"), None, None),
            P(("group", "temp")),
            P(("group", "temp")),
            P(("group", "temp"), "gz", None, None),
            P(("group", "temp"), "gz", None, None),
            P(("group", "temp"), "gz", None, None),
            P(("group", "temp")),
        ),
        out_specs=(P(("group", "temp"), None, "gz", None, None), P(("group", "temp"))),
        check_vma=False,
    )
```

time: 98.2 us -> 88.9 us (0.905)
  starting transfers between devices: 48.9 us -> 44.5 us
  waiting for transfers between devices: 16 us -> 13.8 us
  Pallas kernels: 14.6 us -> 13.1 us
    ppermute x6, starting transfers between devices: 16.7 us -> 9.19 us  [away(): return lax.ppermute(value, 'temp', partners[u])]
    ppermute x6, waiting for transfers between devices: 8.08 us -> 4.93 us  [away(): return lax.ppermute(value, 'temp', partners[u])]
    ppermute x7, starting transfers between devices: 0.02 us -> 1.87 us  [swap_in(): return lax.ppermute(value, 'gz', in_chip)]
    ppermute x7, starting transfers between devices: 32.2 us -> 33.5 us  [swap_cross(): return lax.ppermute(value, 'gz', cross)]
    pallas_call x1, Pallas kernels: 2.58 us -> 1.42 us  [step(): kernel_call(functools.partial(out_kernel, planes, half), [jax.ShapeDtypeS...]
    pallas_call x10 -> x16, Pallas kernels: 8.91 us -> 8.59 us  [the longest x4 2.49 us: step(): kernel_call(functools.partial(relax_early, planes, half, first), [vm(3 *...]
  transfers between devices with their start and end apart: 20 -> 20, of which waited for: 4 -> 8; matrix products, arithmetic and copies ran while one was open for 1% -> 1% of each run, Pallas kernels for 11% -> 11%
where the time goes in v1:
time: 88.9 us; the launch traced here: 88.7 us
  starting transfers between devices  44.5 us (50%)
  blocking collectives  15.6 us (18%)
  waiting for transfers between devices  13.8 us (16%)
  Pallas kernels  13.1 us (15%)
  between operations  0.96 us (1%)
    ppermute x7, starting transfers between devices, swap_cross(): return lax.ppermute(value, 'gz', cross)  33.5 us
    all_to_all x1, blocking collectives, step(): lax.all_to_all(energy[0], 'gz', split_axis=0, concat_axis=0, tiled=True)  15.6 us
    ppermute x6, starting transfers between devices, away(): return lax.ppermute(value, 'temp', partners[u])  9.19 us
    ppermute x7, waiting for transfers between devices, swap_cross(): return lax.ppermute(value, 'gz', cross)  7.87 us
    ppermute x6, waiting for transfers between devices, away(): return lax.ppermute(value, 'temp', partners[u])  4.93 us
    pallas_call x4, Pallas kernels, step(): kernel_call(functools.partial(relax_early, planes, half, first), [vm(3 *...  2.49 us
    pallas_call x2, Pallas kernels, step(): kernel_call(functools.partial(heat_early, planes, half, u), [vm(EARLY * h...  1.92 us
    pallas_call x4, Pallas kernels, step(): kernel_call(functools.partial(relax_late, planes, half, first), [pair] *...  1.89 us
  transfers between devices with their start and end apart: 20, of which 8 were waited for; matrix products, arithmetic and copies ran while one was open for 1% of the time, Pallas kernels for 11%

profile of v1, /device:TPU:40, one launch (start us, length us, event | category | flops | bytes accessed | tf_op | source)
XLA Modules:
  0.0 88.7 jit_solution(17254654763373506125)
XLA Ops:
  0.6 1.7 %shard_map.95 = (f32[1088,128]{1,0:T(8,128)S(1)}, f32[1088,128]{1,0:T(8,128)S(1)}, f32[576,128]{1,0:T(8,128)S(1)}, f32[576,128]{1,0:T(8,128)S(1)}, f32[384,128]{...) custom-call(s32[2]{0:T(128)} %swap.1, s32[2]{0:T(128)} %colour.1, ...), custom_call_target="tpu_custom_call" | custom-call | tf_op jit(solution)/shard_map/pallas_call | solution.py:519
  2.5 22.5 %collective-permute-start.1 = (f32[1088,128]{1,0:T(8,128)S(1)}, f32[1088,128]{1,0:T(8,128)S(1)}, u32[]{:S(2)}, u32[]{:S(2)}) collective-permute-start(f32[1088,128]{1,0:T(8,128)S(1)} %get-tuple-element.47.refs_2_.refs_3_), channel_id=1, source_target_pairs={{0,31},{1,2},{2,1},{3,4},{4,3},{5,6},{6,5},{7,8},{8,7},{9,10},{10,... | collective-permute-start | bytes 1671176 | tf_op jit(solution)/shard_map/ppermute | solution.py:511
  25.5 1.0 %collective-permute-done.7.refs_4_ = f32[576,128]{1,0:T(8,128)S(1)} collective-permute-done((f32[576,128]{1,0:T(8,128)S(1)}, f32[576,128]{1,0:T(8,128)S(1)}, u32[]{:S(2)}, u32[]{:S(2)}) %collective-permute-start.7) | collective-permute-done | bytes 294944 | tf_op jit(solution)/shard_map/ppermute | solution.py:508
  28.7 1.4 %shard_map.102 = (f32[4,4,64,128]{3,2,1,0:T(8,128)S(1)}, f32[4,4,64,128]{3,2,1,0:T(8,128)S(1)}, f32[4,4,64,128]{3,2,1,0:T(8,128)S(1)}, f32[4,4,64,128]{3,2,1,0:T...) custom-call(s32[2]{0:T(128)S(1)} %copy-done.4, s32[2]{0:T(128)S(1)} %copy-done.5, ...), custom_call_target="tpu_custom_call" | custom-call | tf_op jit(solution)/shard_map/pallas_call | solution.py:540
  30.2 2.0 %collective-permute-done.1.refs_1_.refs_4_ = f32[1088,128]{1,0:T(8,128)S(1)} collective-permute-done((f32[1088,128]{1,0:T(8,128)S(1)}, f32[1088,128]{1,0:T(8,128)S(1)}, u32[]{:S(2)}, u32[]{:S(2)}) %collective-permute-start.1) | collective-permute-done | bytes 557088 | tf_op jit(solution)/shard_map/ppermute | solution.py:511
  32.8 3.1 %collective-permute-start.2 = (f32[384,128]{1,0:T(8,128)S(1)}, f32[384,128]{1,0:T(8,128)S(1)}, u32[]{:S(2)}, u32[]{:S(2)}) collective-permute-start(f32[384,128]{1,0:T(8,128)S(1)} %get-tuple-element.51.refs_2_.refs_3_), channel_id=1, source_target_pairs={{0,31},{1,2},{2,1},{3,4},{4,3},{5,6},{6,5},{7,8},{8,7},{9,10},{10,... | collective-permute-start | bytes 589832 | tf_op jit(solution)/shard_map/ppermute | solution.py:511
  36.4 2.5 %collective-permute-start.8 = (f32[384,128]{1,0:T(8,128)S(1)}, f32[384,128]{1,0:T(8,128)S(1)}, u32[]{:S(2)}, u32[]{:S(2)}) collective-permute-start(f32[384,128]{1,0:T(8,128)S(1)} %get-tuple-element.67.refs_2_.refs_3_), channel_id=1, source_target_pairs={{0,31},{1,2},{2,1},{3,4},{4,3},{5,6},{6,5},{7,8},{8,7},{9,10},{10,... | collective-permute-start | bytes 589832 | tf_op jit(solution)/shard_map/ppermute | solution.py:511
  41.6 1.2 %collective-permute-done.8.refs_4_ = f32[384,128]{1,0:T(8,128)S(1)} collective-permute-done((f32[384,128]{1,0:T(8,128)S(1)}, f32[384,128]{1,0:T(8,128)S(1)}, u32[]{:S(2)}, u32[]{:S(2)}) %collective-permute-start.8) | collective-permute-done | bytes 196640 | tf_op jit(solution)/shard_map/ppermute | solution.py:511
  43.3 1.0 %shard_map.108 = (f32[968,128]{1,0:T(8,128)S(1)}, f32[64,128]{1,0:T(8,128)S(1)}) custom-call(s32[8,128]{1,0:T(8,128)S(1)} %get-tuple-element.43.refs_3_.refs_0_.refs_1_.info1, f32[8,128]{1,0:T(8,128)S(1)} %get-tuple-element.60.refs_1_, f32[2,4,6,64,128]{4,3,2,1,0:T(8,128)S(1)} %get-tuple-element.61.refs_1_.refs_2_, ...), custom_call_target="tpu_custom_call" | custom-call | tf_op jit(solution)/shard_map/pallas_call | solution.py:582
  44.2 3.3 %collective-permute-start.15 = (f32[968,128]{1,0:T(8,128)S(1)}, f32[968,128]{1,0:T(8,128)S(1)}, u32[]{:S(2)}, u32[]{:S(2)}) collective-permute-start(f32[968,128]{1,0:T(8,128)S(1)} %get-tuple-element.74.refs_9_.refs_3_), channel_id=1, source_target_pairs={{0,96},{32,64},{64,32},{96,0},{1,97},{33,65},{65,33},{97,1},{2,98}... | collective-permute-start | bytes 1486856 | tf_op jit(solution)/shard_map/ppermute | solution.py:514
  47.5 1.0 %shard_map.103 = (f32[968,128]{1,0:T(8,128)S(1)}, f32[64,128]{1,0:T(8,128)S(1)}) custom-call(s32[8,128]{1,0:T(8,128)S(1)} %get-tuple-element.42.refs_2_.refs_0_.info0, f32[8,128]{1,0:T(8,128)S(1)} %get-tuple-element.44.refs_1_, f32[2,4,6,64,128]{4,3,2,1,0:T(8,128)S(1)} %get-tuple-element.46.refs_1_.refs_2_, f32[384,128]{1,0:T(8,128)S(1)} %shard_map.101.refs_3_.refs_4_, ...), custom_call_target="tpu_custom_call" | custom-call | tf_op jit(solution)/shard_map/pallas_call | solution.py:582
  48.7 2.2 %collective-permute-start.12 = (f32[384,128]{1,0:T(8,128)S(1)}, f32[384,128]{1,0:T(8,128)S(1)}, u32[]{:S(2)}, u32[]{:S(2)}) collective-permute-start(f32[384,128]{1,0:T(8,128)S(1)} %get-tuple-element.75), channel_id=1, source_target_pairs={{0,31},{1,2},{2,1},{3,4},{4,3},{5,6},{6,5},{7,8},{8,7},{9,10},{10,... | collective-permute-start | bytes 589832 | tf_op jit(solution)/shard_map/ppermute | solution.py:511
  51.7 2.1 %collective-permute-start.13 = (f32[384,128]{1,0:T(8,128)S(1)}, f32[384,128]{1,0:T(8,128)S(1)}, u32[]{:S(2)}, u32[]{:S(2)}) collective-permute-start(f32[384,128]{1,0:T(8,128)S(1)} %shard_map.107.refs_3_.refs_4_), channel_id=1, source_target_pairs={{0,31},{1,2},{2,1},{3,4},{4,3},{5,6},{6,5},{7,8},{8,7},{9,10},{10,... | collective-permute-start | bytes 589832 | tf_op jit(solution)/shard_map/ppermute | solution.py:511
  53.8 1.2 %collective-permute-done.12.refs_8_ = f32[384,128]{1,0:T(8,128)S(1)} collective-permute-done((f32[384,128]{1,0:T(8,128)S(1)}, f32[384,128]{1,0:T(8,128)S(1)}, u32[]{:S(2)}, u32[]{:S(2)}) %collective-permute-start.12) | collective-permute-done | bytes 196640 | tf_op jit(solution)/shard_map/ppermute | solution.py:511
  55.1 2.1 %collective-permute-done.11.refs_5_ = f32[384,128]{1,0:T(8,128)S(1)} collective-permute-done((f32[384,128]{1,0:T(8,128)S(1)}, f32[384,128]{1,0:T(8,128)S(1)}, u32[]{:S(2)}, u32[]{:S(2)}) %collective-permute-start.11) | collective-permute-done | bytes 196640 | tf_op jit(solution)/shard_map/ppermute | solution.py:511
  57.9 1.3 %collective-permute-done.13.refs_5_ = f32[384,128]{1,0:T(8,128)S(1)} collective-permute-done((f32[384,128]{1,0:T(8,128)S(1)}, f32[384,128]{1,0:T(8,128)S(1)}, u32[]{:S(2)}, u32[]{:S(2)}) %collective-permute-start.13) | collective-permute-done | bytes 196640 | tf_op jit(solution)/shard_map/ppermute | solution.py:511
  60.0 1.1 %collective-permute-start.17 = (f32[576,128]{1,0:T(8,128)S(1)}, f32[576,128]{1,0:T(8,128)S(1)}, u32[]{:S(2)}, u32[]{:S(2)}) collective-permute-start(f32[576,128]{1,0:T(8,128)S(1)} %get-tuple-element.80.refs_5_), channel_id=1, source_target_pairs={{0,96},{32,64},{64,32},{96,0},{1,97},{33,65},{65,33},{97,1},{2,98}... | collective-permute-start | bytes 884744 | tf_op jit(solution)/shard_map/ppermute | solution.py:514
  61.1 1.1 %collective-permute-start.16 = (f32[576,128]{1,0:T(8,128)S(1)}, f32[576,128]{1,0:T(8,128)S(1)}, u32[]{:S(2)}, u32[]{:S(2)}) collective-permute-start(f32[576,128]{1,0:T(8,128)S(1)} %get-tuple-element.77.refs_4_), channel_id=1, source_target_pairs={{0,32},{32,0},{64,96},{96,64},{1,33},{33,1},{65,97},{97,65},{2,34}... | collective-permute-start | bytes 884744 | tf_op jit(solution)/shard_map/ppermute | solution.py:514
  62.2 15.6 %all_to_all.11 = f32[32,1,2]{2,1,0:T(1,128)S(1)} all-to-all(f32[32,1,2]{2,1,0:T(1,128)S(1)} %bitcast.7), channel_id=1, replica_groups=mesh['group'=2,'temp'=4,'gz'=32] {'gz'}, dimensions={0} | all-to-all | bytes 512 | tf_op jit(solution)/shard_map/all_to_all | solution.py:602
  77.8 1.1 %collective-permute-start.18 = (f32[1,2]{1,0:T(1,128)S(1)}, f32[1,2]{1,0:T(1,128)S(1)}, u32[]{:S(2)}, u32[]{:S(2)}) collective-permute-start(f32[1,2]{1,0:T(1,128)S(1)} %shard_map.112.total), channel_id=1, source_target_pairs={{0,32},{32,0},{64,96},{96,64},{1,33},{33,1},{65,97},{97,65},{2,34}... | collective-permute-start | bytes 32 | tf_op jit(solution)/shard_map/ppermute | solution.py:514
  78.9 2.6 %collective-permute-done.18.r0 = f32[1,2]{1,0:T(1,128)S(1)} collective-permute-done((f32[1,2]{1,0:T(1,128)S(1)}, f32[1,2]{1,0:T(1,128)S(1)}, u32[]{:S(2)}, u32[]{:S(2)}) %collective-permute-start.18) | collective-permute-done | bytes 40 | tf_op jit(solution)/shard_map/ppermute | solution.py:514
  81.5 2.5 %collective-permute-start.19 = (f32[1,2]{1,0:T(1,128)S(1)}, f32[1,2]{1,0:T(1,128)S(1)}, u32[]{:S(2)}, u32[]{:S(2)}) collective-permute-start(f32[1,2]{1,0:T(1,128)S(1)} %shard_map.112.total), channel_id=1, source_target_pairs={{0,96},{32,64},{64,32},{96,0},{1,97},{33,65},{65,33},{97,1},{2,98}... | collective-permute-start | bytes 32 | tf_op jit(solution)/shard_map/ppermute | solution.py:514
  84.0 2.3 %collective-permute-done.19.r1 = f32[1,2]{1,0:T(1,128)S(1)} collective-permute-done((f32[1,2]{1,0:T(1,128)S(1)}, f32[1,2]{1,0:T(1,128)S(1)}, u32[]{:S(2)}, u32[]{:S(2)}) %collective-permute-start.19) | collective-permute-done | bytes 40 | tf_op jit(solution)/shard_map/ppermute | solution.py:514
  87.2 1.4 %shard_map.111 = f32[2,3,4,128,128]{4,3,2,1,0:T(8,128)} custom-call(s32[8,128]{1,0:T(8,128)S(1)} %get-tuple-element.42.refs_2_.refs_0_.info0, s32[8,128]{1,0:T(8,128)S(1)} %get-tuple-element.43.refs_3_.refs_0_.refs_1_.info1, f32[968,128]{1,0:T(8,128)S(1)} %get-tuple-element.59.refs_9_.refs_2_, f32[968,128]{1,0:T(8,128)S(1)} %get-tuple-element.74.refs_9_.refs_3_, ...), custom_call_target="tpu_custom_call" | custom-call | tf_op jit(solution)/shard_map/pallas_call | solution.py:608
  (49 shorter events, 10.7 us)
Async XLA Ops:
  0.6 24.6 %copy-start = (f32[3,4,128,128]{3,2,1,0:T(8,128)S(1)}, f32[3,4,128,128]{3,2,1,0:T(8,128)}, u32[]{:S(2)}) copy-start(f32[3,4,128,128]{3,2,1,0:T(8,128)} %refs_0_.5) | copy-start | bytes 2359300
  2.3 22.9 %collective-permute-start = (f32[1088,128]{1,0:T(8,128)S(1)}, f32[1088,128]{1,0:T(8,128)S(1)}, u32[]{:S(2)}, u32[]{:S(2)}) collective-permute-start(f32[1088,128]{1,0:T(8,128)S(1)} %get-tuple-element.45.refs_3_), channel_id=1, source_target_pairs={{0,1},{1,0},{2,3},{3,2},{4,5},{5,4},{6,7},{7,6},{8,9},{9,8},{10,11... | collective-permute-start | bytes 1671176 | tf_op jit(solution)/shard_map/ppermute | solution.py:508
  2.5 29.7 %collective-permute-start.1 = (f32[1088,128]{1,0:T(8,128)S(1)}, f32[1088,128]{1,0:T(8,128)S(1)}, u32[]{:S(2)}, u32[]{:S(2)}) collective-permute-start(f32[1088,128]{1,0:T(8,128)S(1)} %get-tuple-element.47.refs_2_.refs_3_), channel_id=1, source_target_pairs={{0,31},{1,2},{2,1},{3,4},{4,3},{5,6},{6,5},{7,8},{8,7},{9,10},{10,... | collective-permute-start | bytes 1671176 | tf_op jit(solution)/shard_map/ppermute | solution.py:511
  24.9 1.6 %collective-permute-start.7 = (f32[576,128]{1,0:T(8,128)S(1)}, f32[576,128]{1,0:T(8,128)S(1)}, u32[]{:S(2)}, u32[]{:S(2)}) collective-permute-start(f32[576,128]{1,0:T(8,128)S(1)} %get-tuple-element.64.refs_3_), channel_id=1, source_target_pairs={{0,1},{1,0},{2,3},{3,2},{4,5},{5,4},{6,7},{7,6},{8,9},{9,8},{10,11... | collective-permute-start | bytes 884744 | tf_op jit(solution)/shard_map/ppermute | solution.py:508
  24.9 10.9 %collective-permute-start.6 = (f32[576,128]{1,0:T(8,128)S(1)}, f32[576,128]{1,0:T(8,128)S(1)}, u32[]{:S(2)}, u32[]{:S(2)}) collective-permute-start(f32[576,128]{1,0:T(8,128)S(1)} %get-tuple-element.63.refs_2_.refs_3_), channel_id=1, source_target_pairs={{0,31},{1,2},{2,1},{3,4},{4,3},{5,6},{6,5},{7,8},{8,7},{9,10},{10,... | collective-permute-start | bytes 884744 | tf_op jit(solution)/shard_map/ppermute | solution.py:511
  27.1 11.8 %collective-permute-start.9 = (f32[384,128]{1,0:T(8,128)S(1)}, f32[384,128]{1,0:T(8,128)S(1)}, u32[]{:S(2)}, u32[]{:S(2)}) collective-permute-start(f32[384,128]{1,0:T(8,128)S(1)} %get-tuple-element.68.refs_3_), channel_id=1, source_target_pairs={{0,1},{1,0},{2,3},{3,2},{4,5},{5,4},{6,7},{7,6},{8,9},{9,8},{10,11... | collective-permute-start | bytes 589832 | tf_op jit(solution)/shard_map/ppermute | solution.py:508
  27.4 1.4 %copy-start.3 = (f32[2,4,128,128]{3,2,1,0:T(8,128)S(1)}, f32[2,4,128,128]{3,2,1,0:T(8,128)}, u32[]{:S(2)}) copy-start(f32[2,4,128,128]{3,2,1,0:T(8,128)} %angle.1) | copy-start | bytes 1572868
  27.4 1.4 %copy-start.4 = (s32[2]{0:T(128)S(1)}, s32[2]{0:T(128)}, u32[]{:S(2)}) copy-start(s32[2]{0:T(128)} %swap.1) | copy-start | bytes 28
  27.4 1.4 %copy-start.5 = (s32[2]{0:T(128)S(1)}, s32[2]{0:T(128)}, u32[]{:S(2)}) copy-start(s32[2]{0:T(128)} %colour.1) | copy-start | bytes 28
  28.0 12.1 %collective-permute-start.3 = (f32[384,128]{1,0:T(8,128)S(1)}, f32[384,128]{1,0:T(8,128)S(1)}, u32[]{:S(2)}, u32[]{:S(2)}) collective-permute-start(f32[384,128]{1,0:T(8,128)S(1)} %get-tuple-element.52.refs_3_), channel_id=1, source_target_pairs={{0,1},{1,0},{2,3},{3,2},{4,5},{5,4},{6,7},{7,6},{8,9},{9,8},{10,11... | collective-permute-start | bytes 589832 | tf_op jit(solution)/shard_map/ppermute | solution.py:508
  32.8 8.3 %collective-permute-start.2 = (f32[384,128]{1,0:T(8,128)S(1)}, f32[384,128]{1,0:T(8,128)S(1)}, u32[]{:S(2)}, u32[]{:S(2)}) collective-permute-start(f32[384,128]{1,0:T(8,128)S(1)} %get-tuple-element.51.refs_2_.refs_3_), channel_id=1, source_target_pairs={{0,31},{1,2},{2,1},{3,4},{4,3},{5,6},{6,5},{7,8},{8,7},{9,10},{10,... | collective-permute-start | bytes 589832 | tf_op jit(solution)/shard_map/ppermute | solution.py:511
  36.4 6.4 %collective-permute-start.8 = (f32[384,128]{1,0:T(8,128)S(1)}, f32[384,128]{1,0:T(8,128)S(1)}, u32[]{:S(2)}, u32[]{:S(2)}) collective-permute-start(f32[384,128]{1,0:T(8,128)S(1)} %get-tuple-element.67.refs_2_.refs_3_), channel_id=1, source_target_pairs={{0,31},{1,2},{2,1},{3,4},{4,3},{5,6},{6,5},{7,8},{8,7},{9,10},{10,... | collective-permute-start | bytes 589832 | tf_op jit(solution)/shard_map/ppermute | solution.py:511
  38.9 4.4 %collective-permute-start.5 = (f32[384,128]{1,0:T(8,128)S(1)}, f32[384,128]{1,0:T(8,128)S(1)}, u32[]{:S(2)}, u32[]{:S(2)}) collective-permute-start(f32[384,128]{1,0:T(8,128)S(1)} %get-tuple-element.58), channel_id=1, source_target_pairs={{0,1},{1,0},{2,3},{3,2},{4,5},{5,4},{6,7},{7,6},{8,9},{9,8},{10,11... | collective-permute-start | bytes 589832 | tf_op jit(solution)/shard_map/ppermute | solution.py:508
  39.5 3.8 %collective-permute-start.10 = (f32[384,128]{1,0:T(8,128)S(1)}, f32[384,128]{1,0:T(8,128)S(1)}, u32[]{:S(2)}, u32[]{:S(2)}) collective-permute-start(f32[384,128]{1,0:T(8,128)S(1)} %get-tuple-element.71.refs_4_), channel_id=1, source_target_pairs={{0,1},{1,0},{2,3},{3,2},{4,5},{5,4},{6,7},{7,6},{8,9},{9,8},{10,11... | collective-permute-start | bytes 589832 | tf_op jit(solution)/shard_map/ppermute | solution.py:508
  40.8 6.7 %collective-permute-start.4 = (f32[384,128]{1,0:T(8,128)S(1)}, f32[384,128]{1,0:T(8,128)S(1)}, u32[]{:S(2)}, u32[]{:S(2)}) collective-permute-start(f32[384,128]{1,0:T(8,128)S(1)} %get-tuple-element.55.refs_4_), channel_id=1, source_target_pairs={{0,1},{1,0},{2,3},{3,2},{4,5},{5,4},{6,7},{7,6},{8,9},{9,8},{10,11... | collective-permute-start | bytes 589832 | tf_op jit(solution)/shard_map/ppermute | solution.py:508
  44.2 42.1 %collective-permute-start.15 = (f32[968,128]{1,0:T(8,128)S(1)}, f32[968,128]{1,0:T(8,128)S(1)}, u32[]{:S(2)}, u32[]{:S(2)}) collective-permute-start(f32[968,128]{1,0:T(8,128)S(1)} %get-tuple-element.74.refs_9_.refs_3_), channel_id=1, source_target_pairs={{0,96},{32,64},{64,32},{96,0},{1,97},{33,65},{65,33},{97,1},{2,98}... | collective-permute-start | bytes 1486856 | tf_op jit(solution)/shard_map/ppermute | solution.py:514
  48.5 37.8 %collective-permute-start.14 = (f32[968,128]{1,0:T(8,128)S(1)}, f32[968,128]{1,0:T(8,128)S(1)}, u32[]{:S(2)}, u32[]{:S(2)}) collective-permute-start(f32[968,128]{1,0:T(8,128)S(1)} %get-tuple-element.59.refs_9_.refs_2_), channel_id=1, source_target_pairs={{0,32},{32,0},{64,96},{96,64},{1,33},{33,1},{65,97},{97,65},{2,34}... | collective-permute-start | bytes 1486856 | tf_op jit(solution)/shard_map/ppermute | solution.py:514
  48.7 6.4 %collective-permute-start.12 = (f32[384,128]{1,0:T(8,128)S(1)}, f32[384,128]{1,0:T(8,128)S(1)}, u32[]{:S(2)}, u32[]{:S(2)}) collective-permute-start(f32[384,128]{1,0:T(8,128)S(1)} %get-tuple-element.75), channel_id=1, source_target_pairs={{0,31},{1,2},{2,1},{3,4},{4,3},{5,6},{6,5},{7,8},{8,7},{9,10},{10,... | collective-permute-start | bytes 589832 | tf_op jit(solution)/shard_map/ppermute | solution.py:511
  50.9 6.3 %collective-permute-start.11 = (f32[384,128]{1,0:T(8,128)S(1)}, f32[384,128]{1,0:T(8,128)S(1)}, u32[]{:S(2)}, u32[]{:S(2)}) collective-permute-start(f32[384,128]{1,0:T(8,128)S(1)} %shard_map.101.refs_3_.refs_4_), channel_id=1, source_target_pairs={{0,31},{1,2},{2,1},{3,4},{4,3},{5,6},{6,5},{7,8},{8,7},{9,10},{10,... | collective-permute-start | bytes 589832 | tf_op jit(solution)/shard_map/ppermute | solution.py:511
  51.7 7.6 %collective-permute-start.13 = (f32[384,128]{1,0:T(8,128)S(1)}, f32[384,128]{1,0:T(8,128)S(1)}, u32[]{:S(2)}, u32[]{:S(2)}) collective-permute-start(f32[384,128]{1,0:T(8,128)S(1)} %shard_map.107.refs_3_.refs_4_), channel_id=1, source_target_pairs={{0,31},{1,2},{2,1},{3,4},{4,3},{5,6},{6,5},{7,8},{8,7},{9,10},{10,... | collective-permute-start | bytes 589832 | tf_op jit(solution)/shard_map/ppermute | solution.py:511
  60.0 27.1 %collective-permute-start.17 = (f32[576,128]{1,0:T(8,128)S(1)}, f32[576,128]{1,0:T(8,128)S(1)}, u32[]{:S(2)}, u32[]{:S(2)}) collective-permute-start(f32[576,128]{1,0:T(8,128)S(1)} %get-tuple-element.80.refs_5_), channel_id=1, source_target_pairs={{0,96},{32,64},{64,32},{96,0},{1,97},{33,65},{65,33},{97,1},{2,98}... | collective-permute-start | bytes 884744 | tf_op jit(solution)/shard_map/ppermute | solution.py:514
  61.1 26.1 %collective-permute-start.16 = (f32[576,128]{1,0:T(8,128)S(1)}, f32[576,128]{1,0:T(8,128)S(1)}, u32[]{:S(2)}, u32[]{:S(2)}) collective-permute-start(f32[576,128]{1,0:T(8,128)S(1)} %get-tuple-element.77.refs_4_), channel_id=1, source_target_pairs={{0,32},{32,0},{64,96},{96,64},{1,33},{33,1},{65,97},{97,65},{2,34}... | collective-permute-start | bytes 884744 | tf_op jit(solution)/shard_map/ppermute | solution.py:514
  77.8 3.7 %collective-permute-start.18 = (f32[1,2]{1,0:T(1,128)S(1)}, f32[1,2]{1,0:T(1,128)S(1)}, u32[]{:S(2)}, u32[]{:S(2)}) collective-permute-start(f32[1,2]{1,0:T(1,128)S(1)} %shard_map.112.total), channel_id=1, source_target_pairs={{0,32},{32,0},{64,96},{96,64},{1,33},{33,1},{65,97},{97,65},{2,34}... | collective-permute-start | bytes 32 | tf_op jit(solution)/shard_map/ppermute | solution.py:514
  81.5 4.8 %collective-permute-start.19 = (f32[1,2]{1,0:T(1,128)S(1)}, f32[1,2]{1,0:T(1,128)S(1)}, u32[]{:S(2)}, u32[]{:S(2)}) collective-permute-start(f32[1,2]{1,0:T(1,128)S(1)} %shard_map.112.total), channel_id=1, source_target_pairs={{0,96},{32,64},{64,32},{96,0},{1,97},{33,65},{65,33},{97,1},{2,98}... | collective-permute-start | bytes 32 | tf_op jit(solution)/shard_map/ppermute | solution.py:514
  (2 other events, 2.4 us)

commit v2 on v1

--- a/solution.py
+++ b/solution.py
@@ -85,10 +85,29 @@
     return even if w % 2 == 0 else jnp.logical_not(even)
 
 
+def bond_copies(planes, coup, target, base, rows, side_in, sems):
+    core = core_index()
+    top = planes - 1
+    at_top = 1 - core if side_in else core
+    z = at_top * top
+    return [
+        pltpu.make_async_copy(coup.at[d, p], target.at[pl.ds(base + i * rows, rows), :], sems.at[i])
+        for i, (d, p) in enumerate(((0, z), (1, z), (2, at_top * (top - 1)), (2, z)))
+    ]
+
+
+def bond_kernel(planes, coup, out, sems):
+    copies = bond_copies(planes, coup, out, 0, coup.shape[2], False, sems)
+    for copy in copies:
+        copy.start()
+    for copy in copies:
+        copy.wait()
+
+
 def load_kernel(planes, half, *refs):
     (swap_h, colour_h, beta_h, spin_h, coup_h) = refs[:5]
     (p0x, p0i, p1x, p1i, am0, am1, info0, info1, beta0, beta1) = refs[5:15]
-    swap, colour, betas, spin, sems = refs[15:]
+    swap, colour, betas, spin, sems, bond_sems = refs[15:]
     core = core_index()
     columns = spin.shape[-1]
     rows = 2 * half
@@ -102,16 +121,7 @@
         pltpu.make_async_copy(spin_h.at[:, :, w + core * (top - 2 * w)], spin.at[w], sems.at[3 + w])
         for w in range(planes)
     ]
-    bonds = []
-    zx = core * top
-    zi = top - zx
-    for ref, z, near, outer, sem in (
-        (p0x, zx, core * (top - 1), zx, 3 + planes),
-        (p0i, zi, (1 - core) * (top - 1), zi, 7 + planes),
-    ):
-        for i, (d, p) in enumerate(((0, z), (1, z), (2, near), (2, outer))):
-            target = ref.at[pl.ds(PIECES * half + i * rows, rows), :]
-            bonds.append(pltpu.make_async_copy(coup_h.at[d, p], target, sems.at[sem + i]))
+    bonds = bond_copies(planes, coup_h, p0i, PIECES * half, rows, True, bond_sems)
     for copy in scalars + spins + bonds:
         copy.start()
     for copy in scalars:
@@ -157,7 +167,7 @@
     first = core == 0
 
     def sent(i):
-        return folded_rows(sent_ref, PIECES * half + i * rows, half)
+        return folded_rows(sent_ref, (PIECES * half if in_chip else 0) + i * rows, half)
 
     def zbond(m):
         if m in (-1, planes + 1):
@@ -442,13 +452,14 @@
 
 
 def out_kernel(planes, half, *refs):
-    info0, info1, i0, i1, o0, o1, ri0, ri1, ro0, ro1, out_h, out, sems = refs
+    info0, info1, i0, i1, o0, o1, ri0, ri1, ro0, ro1, out_h, taken, out, sems = refs
     core = core_index()
     columns = out.shape[-1]
     pushes = []
     for u, info, own, other in ((0, info0, (i0, o0), (ri0, ro0)), (1, info1, (i1, o1), (ri1, ro1))):
         note = ri0[pl.ds(EARLY * half, 8), :] if u == 0 else ri1[pl.ds(EARLY * half, 8), :]
         take = exchanged(u, info, note)
+        taken[u : u + 1, :] = jnp.full((1, columns), take.astype(jnp.int32), jnp.int32)
 
         def write(early, late, parities):
             even = (lax.broadcasted_iota(jnp.int32, (half, columns), 1) & 1) == jnp.broadcast_to(
@@ -478,14 +489,20 @@
         push.wait()
 
 
-def energy_kernel(half, info0, info1, total, r0, r1, ri0, ri1, energies):
-    final = []
-    for u, info, r, ri in ((0, info0, r0, ri0), (1, info1, r1, ri1)):
-        take = exchanged(u, info, ri[pl.ds(EARLY * half, 8), :])
-        final.append(jnp.where(take, r[...], total[...]))
+def energy_kernel(taken, total, r0, r1, energies_h, energies, sem):
+    final = [
+        jnp.where(taken[u : u + 1, u : u + 1] > 0, r[:, u : u + 1], total[:, u : u + 1])
+        for u, r in ((0, r0), (1, r1))
+    ]
     lane = lax.broadcasted_iota(jnp.int32, energies.shape, 1)
-    sums = [jnp.sum(jnp.where(lane == u, final[u], 0.0)) for u in range(2)]
-    energies[...] = jnp.where(lane == slot_of(0), sums[0], sums[1])
+    energies[...] = jnp.where(
+        lane == slot_of(0),
+        jnp.broadcast_to(final[0], energies.shape),
+        jnp.broadcast_to(final[1], energies.shape),
+    )
+    copy = pltpu.make_async_copy(energies, energies_h, sem)
+    copy.start()
+    copy.wait()
 
 
 def step(
@@ -514,11 +531,17 @@
         return lax.ppermute(value, "temp", partners[u])
 
     spins = PIECES * half
-    both = spins + 4 * rows
     pair = vm(6 * half, columns)
+    (bonds,) = kernel_call(
+        functools.partial(bond_kernel, planes),
+        [vm(4 * rows, columns)],
+        [HBM],
+        scratch=[pltpu.SemaphoreType.DMA((4,))],
+    )(in_hbm(couplings))
+    r_bonds = swap_cross(bonds)
     p0x, p0i, p1x, p1i, am0, am1, info0, info1, beta0, beta1 = kernel_call(
         functools.partial(load_kernel, planes, half),
-        [vm(both, columns)] * 2
+        [vm(spins, columns), vm(spins + 4 * rows, columns)]
         + [vm(spins, columns)] * 2
         + [pair] * 2
         + [vm(8, columns, dtype=jnp.int32)] * 2
@@ -529,7 +552,8 @@
             pltpu.SMEM((replicas,), jnp.int32),
             pltpu.SMEM((replicas,), F32),
             vm(planes, replicas, 3, rows, columns),
-            pltpu.SemaphoreType.DMA((11 + planes,)),
+            pltpu.SemaphoreType.DMA((3 + planes,)),
+            pltpu.SemaphoreType.DMA((4,)),
         ],
     )(*(in_hbm(v) for v in (swap_bits, colour_order, inverse_temps, spin_state, couplings)))
     info, beta = [info0, info1], [beta0, beta1]
@@ -554,7 +578,7 @@
         functools.partial(weight_kernel, planes, half, False),
         [vm(2, 2, 6, half, columns)] * 2,
         [VM] * 4,
-    )(couplings, rx[0], info0, info1)
+    )(couplings, r_bonds, info0, info1)
 
     assert OR_SWEEPS == 2
     for sweep in range(OR_SWEEPS):
@@ -605,16 +629,20 @@
     )(parts)
     r_total = [away(total, u) for u in range(2)]
 
-    (spin_final,) = kernel_call(
+    spin_final, taken = kernel_call(
         functools.partial(out_kernel, planes, half),
-        [jax.ShapeDtypeStruct(spin_state.shape, F32)],
+        [jax.ShapeDtypeStruct(spin_state.shape, F32), vm(8, columns, dtype=jnp.int32)],
         [VM] * 10,
-        out_specs=[ANY],
+        out_specs=[HBM, VM],
         scratch=[vm(*spin_state.shape), pltpu.SemaphoreType.DMA((2,))],
     )(info0, info1, *inner, *outer, *r_inner, *r_outer)
     (energies,) = kernel_call(
-        functools.partial(energy_kernel, half), [vm(1, 2)], [VM] * 7
-    )(info0, info1, total, *r_total, *r_inner)
+        energy_kernel,
+        [jax.ShapeDtypeStruct((1, 2), F32)],
+        [VM] * 4,
+        out_specs=[HBM],
+        scratch=[vm(1, 2), pltpu.SemaphoreType.DMA(())],
+    )(taken, total, *r_total)
     return spin_final, energies.reshape(-1)
 
 

time: 88.9 us -> 88 us (0.990)
  Pallas kernels: 13.1 us -> 14.5 us
  waiting for transfers between devices: 13.8 us -> 12.4 us
    ppermute x6, waiting for transfers between devices: 4.93 us -> 1.05 us  [away(): return lax.ppermute(value, 'temp', partners[u])]
    ppermute x7 -> x8, waiting for transfers between devices: 7.87 us -> 11.4 us  [swap_cross(): return lax.ppermute(value, 'gz', cross)]
    pallas_call x2 -> x3, Pallas kernels: 2 us -> 3.2 us  [the longest x1 1.64 us: step(): kernel_call(functools.partial(load_kernel, planes, half), [vm(spins, colu...]
    ppermute x7, waiting for transfers between devices: 1 us -> 0.02 us  [swap_in(): return lax.ppermute(value, 'gz', in_chip)]
    ppermute x7 -> x8, starting transfers between devices: 33.5 us -> 32.7 us  [swap_cross(): return lax.ppermute(value, 'gz', cross)]
  transfers between devices with their start and end apart: 20 -> 21, of which waited for: 8 -> 7; matrix products, arithmetic and copies ran while one was open for 1% -> 0% of each run, Pallas kernels for 11% -> 14%
where the time goes in v2:
time: 88 us; the launch traced here: 87.8 us
  starting transfers between devices  44.1 us (50%)
  blocking collectives  15.6 us (18%)
  Pallas kernels  14.5 us (16%)
  waiting for transfers between devices  12.4 us (14%)
  between operations  1.04 us (1%)
    ppermute x8, starting transfers between devices, swap_cross(): return lax.ppermute(value, 'gz', cross)  32.7 us
    all_to_all x1, blocking collectives, step(): lax.all_to_all(energy[0], 'gz', split_axis=0, concat_axis=0, tiled=True)  15.6 us
    ppermute x8, waiting for transfers between devices, swap_cross(): return lax.ppermute(value, 'gz', cross)  11.4 us
    ppermute x6, starting transfers between devices, away(): return lax.ppermute(value, 'temp', partners[u])  9 us
    pallas_call x4, Pallas kernels, step(): kernel_call(functools.partial(relax_early, planes, half, first), [vm(3 *...  2.61 us
    ppermute x7, starting transfers between devices, swap_in(): return lax.ppermute(value, 'gz', in_chip)  2.4 us
    pallas_call x4, Pallas kernels, step(): kernel_call(functools.partial(relax_late, planes, half, first), [pair] *...  1.97 us
    pallas_call x2, Pallas kernels, step(): kernel_call(functools.partial(heat_early, planes, half, u), [vm(EARLY * h...  1.9 us
  transfers between devices with their start and end apart: 21, of which 7 were waited for; matrix products, arithmetic and copies ran while one was open for 0% of the time, Pallas kernels for 14%

profile of v2, /device:TPU:40, one launch (start us, length us, event | category | flops | bytes accessed | tf_op | source)
XLA Modules:
  0.0 87.8 jit_solution(3625399477688208000)
XLA Ops:
  0.6 1.6 %shard_map.95 = (f32[576,128]{1,0:T(8,128)S(1)}, f32[1088,128]{1,0:T(8,128)S(1)}, f32[576,128]{1,0:T(8,128)S(1)}, f32[576,128]{1,0:T(8,128)S(1)}, f32[384,128]{1...) custom-call(s32[2]{0:T(128)} %swap.1, s32[2]{0:T(128)} %colour.1, ...), custom_call_target="tpu_custom_call" | custom-call | tf_op jit(solution)/shard_map/pallas_call | solution.py:542
  2.9 22.1 %collective-permute-start.2 = (f32[576,128]{1,0:T(8,128)S(1)}, f32[576,128]{1,0:T(8,128)S(1)}, u32[]{:S(2)}, u32[]{:S(2)}) collective-permute-start(f32[576,128]{1,0:T(8,128)S(1)} %get-tuple-element.50.refs_2_.refs_3_), channel_id=1, source_target_pairs={{0,31},{1,2},{2,1},{3,4},{4,3},{5,6},{6,5},{7,8},{8,7},{9,10},{10,... | collective-permute-start | bytes 884744 | tf_op jit(solution)/shard_map/ppermute | solution.py:528
  25.1 1.0 %shard_map.97 = f32[512,128]{1,0:T(8,128)S(1)} custom-call(f32[3,4,128,128]{3,2,1,0:T(8,128)} %refs_0_.5), custom_call_target="tpu_custom_call" | custom-call | tf_op jit(solution)/shard_map/pallas_call | solution.py:535
  26.1 3.0 %collective-permute-start.1 = (f32[512,128]{1,0:T(8,128)S(1)}, f32[512,128]{1,0:T(8,128)S(1)}, u32[]{:S(2)}, u32[]{:S(2)}) collective-permute-start(f32[512,128]{1,0:T(8,128)S(1)} %shard_map.97), channel_id=1, source_target_pairs={{0,31},{1,2},{2,1},{3,4},{4,3},{5,6},{6,5},{7,8},{8,7},{9,10},{10,... | collective-permute-start | bytes 786440 | tf_op jit(solution)/shard_map/ppermute | solution.py:528
  31.5 1.4 %shard_map.103 = (f32[4,4,64,128]{3,2,1,0:T(8,128)S(1)}, f32[4,4,64,128]{3,2,1,0:T(8,128)S(1)}, f32[4,4,64,128]{3,2,1,0:T(8,128)S(1)}, f32[4,4,64,128]{3,2,1,0:T...) custom-call(s32[2]{0:T(128)S(1)} %copy-done.4, s32[2]{0:T(128)S(1)} %copy-done.5, ...), custom_call_target="tpu_custom_call" | custom-call | tf_op jit(solution)/shard_map/pallas_call | solution.py:564
  33.0 2.5 %collective-permute-done.1.refs_1_ = f32[512,128]{1,0:T(8,128)S(1)} collective-permute-done((f32[512,128]{1,0:T(8,128)S(1)}, f32[512,128]{1,0:T(8,128)S(1)}, u32[]{:S(2)}, u32[]{:S(2)}) %collective-permute-start.1) | collective-permute-done | bytes 262176 | tf_op jit(solution)/shard_map/ppermute | solution.py:528
  36.1 3.1 %collective-permute-start.3 = (f32[384,128]{1,0:T(8,128)S(1)}, f32[384,128]{1,0:T(8,128)S(1)}, u32[]{:S(2)}, u32[]{:S(2)}) collective-permute-start(f32[384,128]{1,0:T(8,128)S(1)} %get-tuple-element.53.refs_2_.refs_3_), channel_id=1, source_target_pairs={{0,31},{1,2},{2,1},{3,4},{4,3},{5,6},{6,5},{7,8},{8,7},{9,10},{10,... | collective-permute-start | bytes 589832 | tf_op jit(solution)/shard_map/ppermute | solution.py:528
  43.0 3.1 %collective-permute-done.9.refs_4_ = f32[384,128]{1,0:T(8,128)S(1)} collective-permute-done((f32[384,128]{1,0:T(8,128)S(1)}, f32[384,128]{1,0:T(8,128)S(1)}, u32[]{:S(2)}, u32[]{:S(2)}) %collective-permute-start.9) | collective-permute-done | bytes 196640 | tf_op jit(solution)/shard_map/ppermute | solution.py:528
  46.6 0.9 %shard_map.109 = (f32[968,128]{1,0:T(8,128)S(1)}, f32[64,128]{1,0:T(8,128)S(1)}) custom-call(s32[8,128]{1,0:T(8,128)S(1)} %get-tuple-element.45.refs_3_.refs_0_.refs_1_, f32[8,128]{1,0:T(8,128)S(1)} %get-tuple-element.62.refs_1_, f32[2,4,6,64,128]{4,3,2,1,0:T(8,128)S(1)} %get-tuple-element.63.refs_1_.refs_2_, f32[384,128]{1,0:T(8,128)S(1)} %shard_map.108.refs_3_.refs_4_, ...), custom_call_target="tpu_custom_call" | custom-call | tf_op jit(solution)/shard_map/pallas_call | solution.py:606
  47.6 3.3 %collective-permute-start.16 = (f32[968,128]{1,0:T(8,128)S(1)}, f32[968,128]{1,0:T(8,128)S(1)}, u32[]{:S(2)}, u32[]{:S(2)}) collective-permute-start(f32[968,128]{1,0:T(8,128)S(1)} %get-tuple-element.76.refs_9_.refs_3_), channel_id=1, source_target_pairs={{0,96},{32,64},{64,32},{96,0},{1,97},{33,65},{65,33},{97,1},{2,98}... | collective-permute-start | bytes 1486856 | tf_op jit(solution)/shard_map/ppermute | solution.py:531
  50.9 1.0 %shard_map.104 = (f32[968,128]{1,0:T(8,128)S(1)}, f32[64,128]{1,0:T(8,128)S(1)}) custom-call(s32[8,128]{1,0:T(8,128)S(1)} %get-tuple-element.44.refs_2_.refs_0_, f32[8,128]{1,0:T(8,128)S(1)} %get-tuple-element.46.refs_1_, f32[2,4,6,64,128]{4,3,2,1,0:T(8,128)S(1)} %get-tuple-element.48.refs_1_.refs_2_, f32[384,128]{1,0:T(8,128)S(1)} %shard_map.102.refs_3_.refs_4_, ...), custom_call_target="tpu_custom_call" | custom-call | tf_op jit(solution)/shard_map/pallas_call | solution.py:606
  52.0 1.3 %collective-permute-start.13 = (f32[384,128]{1,0:T(8,128)S(1)}, f32[384,128]{1,0:T(8,128)S(1)}, u32[]{:S(2)}, u32[]{:S(2)}) collective-permute-start(f32[384,128]{1,0:T(8,128)S(1)} %get-tuple-element.77), channel_id=1, source_target_pairs={{0,31},{1,2},{2,1},{3,4},{4,3},{5,6},{6,5},{7,8},{8,7},{9,10},{10,... | collective-permute-start | bytes 589832 | tf_op jit(solution)/shard_map/ppermute | solution.py:528
  53.3 1.8 %collective-permute-start.12 = (f32[384,128]{1,0:T(8,128)S(1)}, f32[384,128]{1,0:T(8,128)S(1)}, u32[]{:S(2)}, u32[]{:S(2)}) collective-permute-start(f32[384,128]{1,0:T(8,128)S(1)} %shard_map.102.refs_3_.refs_4_), channel_id=1, source_target_pairs={{0,31},{1,2},{2,1},{3,4},{4,3},{5,6},{6,5},{7,8},{8,7},{9,10},{10,... | collective-permute-start | bytes 589832 | tf_op jit(solution)/shard_map/ppermute | solution.py:528
  55.1 1.2 %collective-permute-start.14 = (f32[384,128]{1,0:T(8,128)S(1)}, f32[384,128]{1,0:T(8,128)S(1)}, u32[]{:S(2)}, u32[]{:S(2)}) collective-permute-start(f32[384,128]{1,0:T(8,128)S(1)} %shard_map.108.refs_3_.refs_4_), channel_id=1, source_target_pairs={{0,31},{1,2},{2,1},{3,4},{4,3},{5,6},{6,5},{7,8},{8,7},{9,10},{10,... | collective-permute-start | bytes 589832 | tf_op jit(solution)/shard_map/ppermute | solution.py:528
  56.3 2.1 %collective-permute-done.13.refs_8_ = f32[384,128]{1,0:T(8,128)S(1)} collective-permute-done((f32[384,128]{1,0:T(8,128)S(1)}, f32[384,128]{1,0:T(8,128)S(1)}, u32[]{:S(2)}, u32[]{:S(2)}) %collective-permute-start.13) | collective-permute-done | bytes 196640 | tf_op jit(solution)/shard_map/ppermute | solution.py:528
  58.4 2.1 %collective-permute-done.12.refs_5_ = f32[384,128]{1,0:T(8,128)S(1)} collective-permute-done((f32[384,128]{1,0:T(8,128)S(1)}, f32[384,128]{1,0:T(8,128)S(1)}, u32[]{:S(2)}, u32[]{:S(2)}) %collective-permute-start.12) | collective-permute-done | bytes 196640 | tf_op jit(solution)/shard_map/ppermute | solution.py:528
  61.3 1.3 %collective-permute-done.14.refs_5_ = f32[384,128]{1,0:T(8,128)S(1)} collective-permute-done((f32[384,128]{1,0:T(8,128)S(1)}, f32[384,128]{1,0:T(8,128)S(1)}, u32[]{:S(2)}, u32[]{:S(2)}) %collective-permute-start.14) | collective-permute-done | bytes 196640 | tf_op jit(solution)/shard_map/ppermute | solution.py:528
  63.4 1.1 %collective-permute-start.18 = (f32[576,128]{1,0:T(8,128)S(1)}, f32[576,128]{1,0:T(8,128)S(1)}, u32[]{:S(2)}, u32[]{:S(2)}) collective-permute-start(f32[576,128]{1,0:T(8,128)S(1)} %get-tuple-element.82.refs_5_), channel_id=1, source_target_pairs={{0,96},{32,64},{64,32},{96,0},{1,97},{33,65},{65,33},{97,1},{2,98}... | collective-permute-start | bytes 884744 | tf_op jit(solution)/shard_map/ppermute | solution.py:531
  64.4 1.1 %collective-permute-start.17 = (f32[576,128]{1,0:T(8,128)S(1)}, f32[576,128]{1,0:T(8,128)S(1)}, u32[]{:S(2)}, u32[]{:S(2)}) collective-permute-start(f32[576,128]{1,0:T(8,128)S(1)} %get-tuple-element.79.refs_4_), channel_id=1, source_target_pairs={{0,32},{32,0},{64,96},{96,64},{1,33},{33,1},{65,97},{97,65},{2,34}... | collective-permute-start | bytes 884744 | tf_op jit(solution)/shard_map/ppermute | solution.py:531
  65.5 15.6 %all_to_all.11 = f32[32,1,2]{2,1,0:T(1,128)S(1)} all-to-all(f32[32,1,2]{2,1,0:T(1,128)S(1)} %bitcast.6), channel_id=1, replica_groups=mesh['group'=2,'temp'=4,'gz'=32] {'gz'}, dimensions={0} | all-to-all | bytes 512 | tf_op jit(solution)/shard_map/all_to_all | solution.py:626
  81.2 1.1 %collective-permute-start.19 = (f32[1,2]{1,0:T(1,128)S(1)}, f32[1,2]{1,0:T(1,128)S(1)}, u32[]{:S(2)}, u32[]{:S(2)}) collective-permute-start(f32[1,2]{1,0:T(1,128)S(1)} %shard_map.113.total), channel_id=1, source_target_pairs={{0,32},{32,0},{64,96},{96,64},{1,33},{33,1},{65,97},{97,65},{2,34}... | collective-permute-start | bytes 32 | tf_op jit(solution)/shard_map/ppermute | solution.py:531
  82.2 2.3 %collective-permute-start.20 = (f32[1,2]{1,0:T(1,128)S(1)}, f32[1,2]{1,0:T(1,128)S(1)}, u32[]{:S(2)}, u32[]{:S(2)}) collective-permute-start(f32[1,2]{1,0:T(1,128)S(1)} %shard_map.113.total), channel_id=1, source_target_pairs={{0,96},{32,64},{64,32},{96,0},{1,97},{33,65},{65,33},{97,1},{2,98}... | collective-permute-start | bytes 32 | tf_op jit(solution)/shard_map/ppermute | solution.py:531
  84.5 1.4 %shard_map.112 = (f32[2,3,4,128,128]{4,3,2,1,0:T(8,128)}, s32[8,128]{1,0:T(8,128)S(1)}) custom-call(s32[8,128]{1,0:T(8,128)S(1)} %get-tuple-element.44.refs_2_.refs_0_, s32[8,128]{1,0:T(8,128)S(1)} %get-tuple-element.45.refs_3_.refs_0_.refs_1_, f32[968,128]{1,0:T(8,128)S(1)} %get-tuple-element.61.refs_9_.refs_2_, ...), custom_call_target="tpu_custom_call" | custom-call | tf_op jit(solution)/shard_map/pallas_call | solution.py:632
  86.0 1.0 %collective-permute-done.20.r1 = f32[1,2]{1,0:T(1,128)S(1)} collective-permute-done((f32[1,2]{1,0:T(1,128)S(1)}, f32[1,2]{1,0:T(1,128)S(1)}, u32[]{:S(2)}, u32[]{:S(2)}) %collective-permute-start.20) | collective-permute-done | bytes 40 | tf_op jit(solution)/shard_map/ppermute | solution.py:531
  (51 shorter events, 10.3 us)
Async XLA Ops:
  0.6 28.5 %copy-start = (f32[3,4,128,128]{3,2,1,0:T(8,128)S(1)}, f32[3,4,128,128]{3,2,1,0:T(8,128)}, u32[]{:S(2)}) copy-start(f32[3,4,128,128]{3,2,1,0:T(8,128)} %refs_0_.5) | copy-start | bytes 2359300
  2.3 26.8 %collective-permute-start = (f32[1088,128]{1,0:T(8,128)S(1)}, f32[1088,128]{1,0:T(8,128)S(1)}, u32[]{:S(2)}, u32[]{:S(2)}) collective-permute-start(f32[1088,128]{1,0:T(8,128)S(1)} %get-tuple-element.47.refs_3_), channel_id=1, source_target_pairs={{0,1},{1,0},{2,3},{3,2},{4,5},{5,4},{6,7},{7,6},{8,9},{9,8},{10,11... | collective-permute-start | bytes 1671176 | tf_op jit(solution)/shard_map/ppermute | solution.py:525
  2.4 27.0 %collective-permute-start.8 = (f32[576,128]{1,0:T(8,128)S(1)}, f32[576,128]{1,0:T(8,128)S(1)}, u32[]{:S(2)}, u32[]{:S(2)}) collective-permute-start(f32[576,128]{1,0:T(8,128)S(1)} %get-tuple-element.66.refs_3_), channel_id=1, source_target_pairs={{0,1},{1,0},{2,3},{3,2},{4,5},{5,4},{6,7},{7,6},{8,9},{9,8},{10,11... | collective-permute-start | bytes 884744 | tf_op jit(solution)/shard_map/ppermute | solution.py:525
  2.9 32.7 %collective-permute-start.2 = (f32[576,128]{1,0:T(8,128)S(1)}, f32[576,128]{1,0:T(8,128)S(1)}, u32[]{:S(2)}, u32[]{:S(2)}) collective-permute-start(f32[576,128]{1,0:T(8,128)S(1)} %get-tuple-element.50.refs_2_.refs_3_), channel_id=1, source_target_pairs={{0,31},{1,2},{2,1},{3,4},{4,3},{5,6},{6,5},{7,8},{8,7},{9,10},{10,... | collective-permute-start | bytes 884744 | tf_op jit(solution)/shard_map/ppermute | solution.py:528
  25.1 14.1 %collective-permute-start.7 = (f32[576,128]{1,0:T(8,128)S(1)}, f32[576,128]{1,0:T(8,128)S(1)}, u32[]{:S(2)}, u32[]{:S(2)}) collective-permute-start(f32[576,128]{1,0:T(8,128)S(1)} %get-tuple-element.65.refs_2_.refs_3_), channel_id=1, source_target_pairs={{0,31},{1,2},{2,1},{3,4},{4,3},{5,6},{6,5},{7,8},{8,7},{9,10},{10,... | collective-permute-start | bytes 884744 | tf_op jit(solution)/shard_map/ppermute | solution.py:528
  26.1 9.4 %collective-permute-start.1 = (f32[512,128]{1,0:T(8,128)S(1)}, f32[512,128]{1,0:T(8,128)S(1)}, u32[]{:S(2)}, u32[]{:S(2)}) collective-permute-start(f32[512,128]{1,0:T(8,128)S(1)} %shard_map.97), channel_id=1, source_target_pairs={{0,31},{1,2},{2,1},{3,4},{4,3},{5,6},{6,5},{7,8},{8,7},{9,10},{10,... | collective-permute-start | bytes 786440 | tf_op jit(solution)/shard_map/ppermute | solution.py:528
  30.0 10.0 %collective-permute-start.10 = (f32[384,128]{1,0:T(8,128)S(1)}, f32[384,128]{1,0:T(8,128)S(1)}, u32[]{:S(2)}, u32[]{:S(2)}) collective-permute-start(f32[384,128]{1,0:T(8,128)S(1)} %get-tuple-element.70.refs_3_), channel_id=1, source_target_pairs={{0,1},{1,0},{2,3},{3,2},{4,5},{5,4},{6,7},{7,6},{8,9},{9,8},{10,11... | collective-permute-start | bytes 589832 | tf_op jit(solution)/shard_map/ppermute | solution.py:525
  30.2 1.3 %copy-start.3 = (f32[2,4,128,128]{3,2,1,0:T(8,128)S(1)}, f32[2,4,128,128]{3,2,1,0:T(8,128)}, u32[]{:S(2)}) copy-start(f32[2,4,128,128]{3,2,1,0:T(8,128)} %angle.1) | copy-start | bytes 1572868
  30.2 1.3 %copy-start.4 = (s32[2]{0:T(128)S(1)}, s32[2]{0:T(128)}, u32[]{:S(2)}) copy-start(s32[2]{0:T(128)} %swap.1) | copy-start | bytes 28
  30.9 10.4 %collective-permute-start.4 = (f32[384,128]{1,0:T(8,128)S(1)}, f32[384,128]{1,0:T(8,128)S(1)}, u32[]{:S(2)}, u32[]{:S(2)}) collective-permute-start(f32[384,128]{1,0:T(8,128)S(1)} %get-tuple-element.54.refs_3_), channel_id=1, source_target_pairs={{0,1},{1,0},{2,3},{3,2},{4,5},{5,4},{6,7},{7,6},{8,9},{9,8},{10,11... | collective-permute-start | bytes 589832 | tf_op jit(solution)/shard_map/ppermute | solution.py:525
  36.1 6.4 %collective-permute-start.3 = (f32[384,128]{1,0:T(8,128)S(1)}, f32[384,128]{1,0:T(8,128)S(1)}, u32[]{:S(2)}, u32[]{:S(2)}) collective-permute-start(f32[384,128]{1,0:T(8,128)S(1)} %get-tuple-element.53.refs_2_.refs_3_), channel_id=1, source_target_pairs={{0,31},{1,2},{2,1},{3,4},{4,3},{5,6},{6,5},{7,8},{8,7},{9,10},{10,... | collective-permute-start | bytes 589832 | tf_op jit(solution)/shard_map/ppermute | solution.py:528
  39.7 6.4 %collective-permute-start.9 = (f32[384,128]{1,0:T(8,128)S(1)}, f32[384,128]{1,0:T(8,128)S(1)}, u32[]{:S(2)}, u32[]{:S(2)}) collective-permute-start(f32[384,128]{1,0:T(8,128)S(1)} %get-tuple-element.69.refs_2_.refs_3_), channel_id=1, source_target_pairs={{0,31},{1,2},{2,1},{3,4},{4,3},{5,6},{6,5},{7,8},{8,7},{9,10},{10,... | collective-permute-start | bytes 589832 | tf_op jit(solution)/shard_map/ppermute | solution.py:528
  39.8 6.8 %collective-permute-start.6 = (f32[384,128]{1,0:T(8,128)S(1)}, f32[384,128]{1,0:T(8,128)S(1)}, u32[]{:S(2)}, u32[]{:S(2)}) collective-permute-start(f32[384,128]{1,0:T(8,128)S(1)} %get-tuple-element.60), channel_id=1, source_target_pairs={{0,1},{1,0},{2,3},{3,2},{4,5},{5,4},{6,7},{7,6},{8,9},{9,8},{10,11... | collective-permute-start | bytes 589832 | tf_op jit(solution)/shard_map/ppermute | solution.py:525
  40.7 5.9 %collective-permute-start.11 = (f32[384,128]{1,0:T(8,128)S(1)}, f32[384,128]{1,0:T(8,128)S(1)}, u32[]{:S(2)}, u32[]{:S(2)}) collective-permute-start(f32[384,128]{1,0:T(8,128)S(1)} %get-tuple-element.73.refs_4_), channel_id=1, source_target_pairs={{0,1},{1,0},{2,3},{3,2},{4,5},{5,4},{6,7},{7,6},{8,9},{9,8},{10,11... | collective-permute-start | bytes 589832 | tf_op jit(solution)/shard_map/ppermute | solution.py:525
  42.0 8.9 %collective-permute-start.5 = (f32[384,128]{1,0:T(8,128)S(1)}, f32[384,128]{1,0:T(8,128)S(1)}, u32[]{:S(2)}, u32[]{:S(2)}) collective-permute-start(f32[384,128]{1,0:T(8,128)S(1)} %get-tuple-element.57.refs_4_), channel_id=1, source_target_pairs={{0,1},{1,0},{2,3},{3,2},{4,5},{5,4},{6,7},{7,6},{8,9},{9,8},{10,11... | collective-permute-start | bytes 589832 | tf_op jit(solution)/shard_map/ppermute | solution.py:525
  47.6 37.0 %collective-permute-start.16 = (f32[968,128]{1,0:T(8,128)S(1)}, f32[968,128]{1,0:T(8,128)S(1)}, u32[]{:S(2)}, u32[]{:S(2)}) collective-permute-start(f32[968,128]{1,0:T(8,128)S(1)} %get-tuple-element.76.refs_9_.refs_3_), channel_id=1, source_target_pairs={{0,96},{32,64},{64,32},{96,0},{1,97},{33,65},{65,33},{97,1},{2,98}... | collective-permute-start | bytes 1486856 | tf_op jit(solution)/shard_map/ppermute | solution.py:531
  51.8 32.7 %collective-permute-start.15 = (f32[968,128]{1,0:T(8,128)S(1)}, f32[968,128]{1,0:T(8,128)S(1)}, u32[]{:S(2)}, u32[]{:S(2)}) collective-permute-start(f32[968,128]{1,0:T(8,128)S(1)} %get-tuple-element.61.refs_9_.refs_2_), channel_id=1, source_target_pairs={{0,32},{32,0},{64,96},{96,64},{1,33},{33,1},{65,97},{97,65},{2,34}... | collective-permute-start | bytes 1486856 | tf_op jit(solution)/shard_map/ppermute | solution.py:531
  52.0 6.4 %collective-permute-start.13 = (f32[384,128]{1,0:T(8,128)S(1)}, f32[384,128]{1,0:T(8,128)S(1)}, u32[]{:S(2)}, u32[]{:S(2)}) collective-permute-start(f32[384,128]{1,0:T(8,128)S(1)} %get-tuple-element.77), channel_id=1, source_target_pairs={{0,31},{1,2},{2,1},{3,4},{4,3},{5,6},{6,5},{7,8},{8,7},{9,10},{10,... | collective-permute-start | bytes 589832 | tf_op jit(solution)/shard_map/ppermute | solution.py:528
  53.3 7.2 %collective-permute-start.12 = (f32[384,128]{1,0:T(8,128)S(1)}, f32[384,128]{1,0:T(8,128)S(1)}, u32[]{:S(2)}, u32[]{:S(2)}) collective-permute-start(f32[384,128]{1,0:T(8,128)S(1)} %shard_map.102.refs_3_.refs_4_), channel_id=1, source_target_pairs={{0,31},{1,2},{2,1},{3,4},{4,3},{5,6},{6,5},{7,8},{8,7},{9,10},{10,... | collective-permute-start | bytes 589832 | tf_op jit(solution)/shard_map/ppermute | solution.py:528
  55.1 7.6 %collective-permute-start.14 = (f32[384,128]{1,0:T(8,128)S(1)}, f32[384,128]{1,0:T(8,128)S(1)}, u32[]{:S(2)}, u32[]{:S(2)}) collective-permute-start(f32[384,128]{1,0:T(8,128)S(1)} %shard_map.108.refs_3_.refs_4_), channel_id=1, source_target_pairs={{0,31},{1,2},{2,1},{3,4},{4,3},{5,6},{6,5},{7,8},{8,7},{9,10},{10,... | collective-permute-start | bytes 589832 | tf_op jit(solution)/shard_map/ppermute | solution.py:528
  63.4 18.9 %collective-permute-start.18 = (f32[576,128]{1,0:T(8,128)S(1)}, f32[576,128]{1,0:T(8,128)S(1)}, u32[]{:S(2)}, u32[]{:S(2)}) collective-permute-start(f32[576,128]{1,0:T(8,128)S(1)} %get-tuple-element.82.refs_5_), channel_id=1, source_target_pairs={{0,96},{32,64},{64,32},{96,0},{1,97},{33,65},{65,33},{97,1},{2,98}... | collective-permute-start | bytes 884744 | tf_op jit(solution)/shard_map/ppermute | solution.py:531
  64.4 20.1 %collective-permute-start.17 = (f32[576,128]{1,0:T(8,128)S(1)}, f32[576,128]{1,0:T(8,128)S(1)}, u32[]{:S(2)}, u32[]{:S(2)}) collective-permute-start(f32[576,128]{1,0:T(8,128)S(1)} %get-tuple-element.79.refs_4_), channel_id=1, source_target_pairs={{0,32},{32,0},{64,96},{96,64},{1,33},{33,1},{65,97},{97,65},{2,34}... | collective-permute-start | bytes 884744 | tf_op jit(solution)/shard_map/ppermute | solution.py:531
  81.2 4.8 %collective-permute-start.19 = (f32[1,2]{1,0:T(1,128)S(1)}, f32[1,2]{1,0:T(1,128)S(1)}, u32[]{:S(2)}, u32[]{:S(2)}) collective-permute-start(f32[1,2]{1,0:T(1,128)S(1)} %shard_map.113.total), channel_id=1, source_target_pairs={{0,32},{32,0},{64,96},{96,64},{1,33},{33,1},{65,97},{97,65},{2,34}... | collective-permute-start | bytes 32 | tf_op jit(solution)/shard_map/ppermute | solution.py:531
  82.2 4.8 %collective-permute-start.20 = (f32[1,2]{1,0:T(1,128)S(1)}, f32[1,2]{1,0:T(1,128)S(1)}, u32[]{:S(2)}, u32[]{:S(2)}) collective-permute-start(f32[1,2]{1,0:T(1,128)S(1)} %shard_map.113.total), channel_id=1, source_target_pairs={{0,96},{32,64},{64,32},{96,0},{1,97},{33,65},{65,33},{97,1},{2,98}... | collective-permute-start | bytes 32 | tf_op jit(solution)/shard_map/ppermute | solution.py:531
  (3 other events, 3.9 us)
